TPU v7x, 32 devices: a whole 2x2x4 slice. The times are simulated.
32 devices in a mesh: chain: 8 (over y, x, core), par: 4 (over z).
Axes of the slice: x: 2, y: 2, z: 4, core: 2. Of those that a mesh axis runs over, the one named last changes fastest.
Arguments:
- propagation_gains: bfloat16 [4, 16, 64, 8192], P('par', None, None, 'chain'), may hold values from -0.13258252 to 0.13258252, as said below
- observed_samples: bfloat16 [4, 16, 32, 8192], P('par', None, None, 'chain'), may hold values from -6 to 6
- disturbance_variance: float32 [4, 16], P(None, 'chain'), may hold values from 0.05 to 0.5
- retained_branches: int32 [4, 16, 16, 1024], P(None, 'chain', 'par'), may hold values from 0 to 63
Outputs:
- distances: float32 [4, 16, 16, 1024], P(None, 'chain', 'par')
Inputs may be any that keep to these rules, and one draw needn't show every extreme that they name: `propagation_gains`: row 2u holds the real and row 2u+1 the imaginary part of the channel to user u.
All inputs are finite; a program needn't handle non-finite values.
Results may differ from a plain program's by a relative error of at most 0.0003.
Values sent between devices are 32-bit elements; how exact they have to be, the bound alone decides.
A program may use at most 64 MiB of HBM per device.

v0:
```python
import functools
import jax
import jax.numpy as jnp
from jax import lax
from jax.experimental import pallas as pl
from jax.experimental.pallas import tpu as pltpu
from jax.sharding import PartitionSpec as P

constellation_norm = 1.0 / 42.0**0.5
LANES = 128
PANEL = 4
MESH = pl.DeviceIdType.MESH
NT = (((1,), (1,)), ((), ()))


def iota(shape, dim):
    return lax.broadcasted_iota(jnp.int32, shape, dim)


def split(x):
    high = x.astype(jnp.bfloat16)
    return high, (x - high.astype(jnp.float32)).astype(jnp.bfloat16)


def pair_swap(x):
    even = iota(x.shape, 1) % 2 == 0
    return jnp.where(even, pltpu.roll(x, LANES - 1, 1), pltpu.roll(x, 1, 1))


def eliminate(mats, users):
    groups = users // 8
    blocks, turned = [], []
    for mat in mats:
        odd = iota((8, LANES), 1) % 2 == 1
        parts = [mat[8 * g : 8 * g + 8, :] for g in range(groups)]
        blocks.append(parts)
        turned.append([jnp.where(odd, pair_swap(p), -pair_swap(p)) for p in parts])
    row = iota((8, LANES), 0)
    for start in range(0, users, PANEL):
        home = start // 8
        panels = [
            [
                {g: jnp.broadcast_to(a[g][:, lane : lane + 1], (8, LANES)) for g in range(home, groups)}
                for lane in range(2 * start, 2 * (start + PANEL))
            ]
            for a in blocks
        ]
        for j in range(start, min(start + PANEL, users - 1)):
            at, c = j % 8, j - start
            for a, ia, panel in zip(blocks, turned, panels):
                real, imag = panel[2 * c], panel[2 * c + 1]
                inverse = 1.0 / real[home][at : at + 1, :]
                pivot_row = a[home][at : at + 1, :] * inverse
                turned_row = ia[home][at : at + 1, :] * inverse
                later = [
                    (d, real[home][at + d - c : at + d - c + 1, :] * inverse, imag[home][at + d - c : at + d - c + 1, :] * inverse)
                    for d in range(c + 1, PANEL)
                ]
                for g in range(home + (at == 7), groups):
                    fr, fi = real[g], imag[g]
                    if g == home:
                        fr, fi = jnp.where(row > at, fr, 0.0), jnp.where(row > at, fi, 0.0)
                    for d, x, y in later:
                        panel[2 * d][g] = panel[2 * d][g] - (fr * x + fi * y)
                        panel[2 * d + 1][g] = panel[2 * d + 1][g] - (fi * x - fr * y)
                    a[g] = a[g] - (fr * pivot_row + fi * turned_row)
                    ia[g] = ia[g] - (fr * turned_row - fi * pivot_row)
    lane, line = iota((users, LANES), 1), iota((users, LANES), 0)
    keep = (lane >= 2 * line) & (lane != 2 * line + 1) | (lane >= 2 * users)
    out = []
    for a in blocks:
        full = jnp.concatenate(a, axis=0)
        pivots = jnp.sum(jnp.where(lane == 2 * line, full, 0.0), axis=1, keepdims=True)
        out.append(jnp.where(keep, full * lax.rsqrt(pivots), 0.0))
    return out


def kernel(
    dims, noise_any, gains_ref, samples_ref, branches_any, out_ref,
    noise_ref, branches_ref, held, raw, part, came, points, packed, taken, rotations,
    small_sem, load_sem, send_sem, recv_sem, usend_sem, urecv_sem,
):
    clusters, bands, users, symbols, share, mine_t, pieces = dims
    copies = LANES // users
    lines = pieces * mine_t
    me, band = lax.axis_index("chain"), lax.axis_index("par")

    barrier = pltpu.get_barrier_semaphore()
    for k in range(1, clusters):
        pl.semaphore_signal(barrier, inc=1, device_id={"chain": lax.rem(me + k, clusters)}, device_id_type=MESH)
    for k in range(1, bands):
        pl.semaphore_signal(barrier, inc=1, device_id={"par": lax.rem(band + k, bands)}, device_id_type=MESH)

    order = list(range(1, clusters)) + [0]
    loads = {}
    for k in order:
        tones = pl.ds(lax.rem(me + k, clusters) * share, share)
        loads[k] = (
            pltpu.make_async_copy(
                gains_ref.at[0, tones], held.at[k, :, pl.ds(0, 2 * users)], load_sem.at[0, k]
            ),
            pltpu.make_async_copy(
                samples_ref.at[0, tones], held.at[k, :, pl.ds(2 * users, 2 * symbols)], load_sem.at[1, k]
            ),
        )
        for copy in loads[k]:
            copy.start()

    small = (
        pltpu.make_async_copy(noise_any, noise_ref, small_sem.at[0]),
        pltpu.make_async_copy(branches_any, branches_ref, small_sem.at[1]),
    )
    for copy in small:
        copy.start()
    raw[...] = jnp.zeros_like(raw)
    even = iota((users, LANES), 1) % 2 == 0
    sends = []
    for number, k in enumerate(order):
        for copy in loads[k]:
            copy.wait()
        for s in range(share):
            slot = (number * share + s) % raw.shape[0]
            both = held[k, s]
            raw[slot, :, : 2 * (users + symbols)] = lax.dot_general(
                both[: 2 * users], both, NT, preferred_element_type=jnp.float32
            )
            on_even = raw[slot, pl.ds(0, users, stride=2), :]
            on_odd = raw[slot, pl.ds(1, users, stride=2), :]
            part[k, s] = pair_swap(on_odd) + jnp.where(even, on_even, -on_even)
        if k:
            if number == 0:
                pl.semaphore_wait(barrier, clusters + bands - 2)
            copy = pltpu.make_async_remote_copy(
                src_ref=part.at[k], dst_ref=came.at[k], send_sem=send_sem.at[k], recv_sem=recv_sem.at[k],
                device_id={"chain": lax.rem(me + k, clusters)}, device_id_type=MESH,
            )
            copy.start()
            sends.append(copy)

    for copy in small:
        copy.wait()
    for b in range(bands):
        for s in range(share):
            q = jnp.concatenate(
                [branches_ref[b, s, :, LANES * r : LANES * (r + 1)] for r in range(pieces)], axis=0
            )
            points[b, s, :, :LANES] = (2 * (q & 7) - 7).astype(jnp.float32).astype(jnp.bfloat16)
            points[b, s, :, LANES:] = (2 * (q >> 3) - 7).astype(jnp.float32).astype(jnp.bfloat16)

    lane, line = iota((users, LANES), 1), iota((users, LANES), 0)
    noises = [
        jnp.sum(jnp.where(iota((1, bands), 1) == band, noise_ref[s : s + 1, :], 0.0), axis=1, keepdims=True)
        for s in range(share)
    ]
    totals = [part[0, s] for s in range(share)]
    for copy in sends:
        copy.wait_recv()
    for k in range(1, clusters):
        totals = [total + came[k, s] for s, total in enumerate(totals)]
    mats = [
        jnp.where(lane == 2 * line, total + noises[s], total) for s, total in enumerate(totals)
    ]
    factors = eliminate(mats, users)

    source, target = iota((LANES, LANES), 0), iota((LANES, LANES), 1) % (2 * users)
    spread = (source == 2 * (target % users) + target // users).astype(jnp.float32).astype(jnp.bfloat16)
    rows = 2 * mine_t
    r, c = iota((bands * rows, LANES), 0), iota((bands * rows, LANES), 1)
    is_odd = (r % rows) // mine_t
    wanted = 2 * users + 2 * ((r // rows) * mine_t + r % mine_t) + is_odd
    pick = jnp.where(c == wanted, (1 - 2 * is_odd).astype(jnp.float32), 0.0).astype(jnp.bfloat16)
    pick = jnp.concatenate([pick, pick], axis=1)
    half = users // 2
    left = iota((half, LANES), 1) < 2 * users
    for s, factor in enumerate(factors):
        high, low = split(factor * constellation_norm)
        wide = jnp.dot(high, spread, preferred_element_type=jnp.float32) + jnp.dot(
            low, spread, preferred_element_type=jnp.float32
        )
        folded = jnp.where(left, wide[:half], wide[half:])
        for k in range(bands):
            packed[k, s, :half] = folded
        high, low = split(factor)
        weights = jnp.concatenate(
            [jnp.concatenate([high] * copies, axis=0), jnp.concatenate([low] * copies, axis=0)], axis=1
        )
        rotations[s] = lax.dot_general(pick, weights, NT, preferred_element_type=jnp.float32)
        for k in range(bands):
            peer = lax.rem(band + k, bands)
            packed[k, s, half:] = rotations[s, pl.ds(pl.multiple_of(peer * rows, rows), rows), :]
    usends = []
    for k in range(1, bands):
        copy = pltpu.make_async_remote_copy(
            src_ref=packed.at[k], dst_ref=taken.at[k], send_sem=usend_sem.at[k], recv_sem=urecv_sem.at[k],
            device_id={"par": lax.rem(band + k, bands)}, device_id_type=MESH,
        )
        copy.start()
        usends.append(copy)

    sr, sc = iota((LANES, LANES), 0), iota((LANES, LANES), 1)
    suffix = jnp.where((sr // users == sc // users) & (sr >= sc), 1.0 / users, 0.0).astype(jnp.bfloat16)
    suffix = jnp.concatenate([suffix, suffix], axis=0)
    lane_block = lane // users
    for k in range(bands):
        if k:
            usends[k - 1].wait_recv()
        b = lax.rem(band + bands - k, bands)
        box = taken if k else packed
        for s in range(share):
            folded = box[k, s, :half]
            crossed = pltpu.roll(folded, 2 * users, 1)
            first = jnp.concatenate(
                [jnp.where(left, folded, crossed), jnp.where(left, crossed, folded)], axis=0
            )
            second = pltpu.roll(first, users, 1)
            ons, offs = [], []
            for i in range(copies):
                here = lane_block == i
                real, imag = (first, second) if i % 2 == 0 else (second, first)
                real, imag = jnp.where(here, real, 0.0), jnp.where(here, imag, 0.0)
                ons.append(jnp.concatenate([real, imag], axis=1))
                offs.append(jnp.concatenate([-imag, real], axis=1))
            high, low = split(jnp.concatenate(ons + offs, axis=0))
            p = points[b, s]
            mapped = lax.dot_general(p, high, NT, preferred_element_type=jnp.float32) + lax.dot_general(
                p, low, NT, preferred_element_type=jnp.float32
            )
            on = jnp.concatenate([box[k, s, half : half + mine_t]] * pieces, axis=0) - mapped[:, :LANES]
            off = jnp.concatenate([box[k, s, half + mine_t :]] * pieces, axis=0) - mapped[:, LANES:]
            high, low = split(on * on + off * off)
            result = jnp.dot(
                jnp.concatenate([high, low], axis=1), suffix, preferred_element_type=jnp.float32
            )
            for r in range(pieces):
                out_ref[b, s, :, LANES * r : LANES * (r + 1)] = result[mine_t * r : mine_t * (r + 1)]
    for copy in sends + usends:
        copy.wait_send()


def local(propagation_gains, observed_samples, disturbance_variance, retained_branches):
    clusters, bands = lax.axis_size("chain"), lax.axis_size("par")
    _, tones, double_users, antennas = propagation_gains.shape
    users, symbols = double_users // 2, observed_samples.shape[2] // 2
    share, mine_t = tones // clusters, symbols // bands
    pieces = retained_branches.shape[-1] // LANES
    dims = (clusters, bands, users, symbols, share, mine_t, pieces)
    f32, bf16 = jnp.float32, jnp.bfloat16
    vmem, dma = pltpu.VMEM, pltpu.SemaphoreType.DMA
    payload = users // 2 + 2 * mine_t
    return pl.pallas_call(
        functools.partial(kernel, dims),
        out_shape=jax.ShapeDtypeStruct(retained_branches.shape, f32),
        in_specs=[
            pl.BlockSpec(memory_space=pl.ANY),
            pl.BlockSpec(memory_space=pl.ANY),
            pl.BlockSpec(memory_space=pl.ANY),
            pl.BlockSpec(memory_space=pl.ANY),
        ],
        out_specs=pl.BlockSpec(memory_space=pltpu.VMEM),
        scratch_shapes=[
            vmem(disturbance_variance.shape[::-1], f32),
            vmem(retained_branches.shape, jnp.int32),
            vmem((clusters, share, 2 * (users + symbols), antennas), bf16),
            vmem((4, 2 * users, LANES), f32),
            vmem((clusters, share, users, LANES), f32),
            vmem((clusters, share, users, LANES), f32),
            vmem((bands, share, pieces * mine_t, 2 * LANES), bf16),
            vmem((bands, share, payload, LANES), f32),
            vmem((bands, share, payload, LANES), f32),
            vmem((share, bands * 2 * mine_t, LANES), f32),
            dma((2,)), dma((2, clusters)), dma((clusters,)), dma((clusters,)), dma((bands,)), dma((bands,)),
        ],
        compiler_params=pltpu.CompilerParams(collective_id=0, has_side_effects=True),
        name="detect",
    )(disturbance_variance.T, propagation_gains, observed_samples, retained_branches)


def solution(mesh):
    placed = (
        P("par", None, None, "chain"),
        P("par", None, None, "chain"),
        P(None, "chain"),
        P(None, "chain", "par", None),
    )
    return jax.shard_map(
        local, mesh=mesh, in_specs=placed, out_specs=P(None, "chain", "par", None), check_vma=False
    )
```

profile of v0, /device:TPU:0, one launch (start us, length us, event | category | flops | bytes accessed | tf_op | source)
XLA Modules:
  0.0 20.4 jit_solution(10498011971807719796)
XLA Ops:
  0.0 18.8 %detect.1 = f32[4,2,4,1024]{3,2,1,0:T(4,128)} custom-call(f32[2,4]{1,0:T(2,128)} %bitcast.1, bf16[1,16,64,1024]{3,2,1,0:T(8,128)(2,1)} %gains_ref.1, bf16[1,16,32,1024]{3,2,1,0:T(8,128)(2,1)} %samples_ref.1, s32[4,2,4,1024]{3,2,1,0:T(4,128)} %branches_any.1), custom_call_target="tpu_custom_call" | custom-call | tf_op jit(solution)/shard_map/detect/pallas_call | solution.py:250
  18.9 1.6 %copy.6 = f32[4,2,4,1024]{3,2,1,0:T(4,128)} copy(f32[4,2,4,1024]{3,2,1,0:T(4,128)} %detect.1) | data formatting | bytes 262144
where the time goes:
time: 20.6 us; the launch traced here: 20.4 us
  Pallas kernels  18.8 us (91%)
  local copies, waits for them, and re-layouts  1.57 us (8%)
    pallas_call x1, Pallas kernels, local(): pl.pallas_call(functools.partial(kernel, dims), out_shape=jax.ShapeDtypeS...  18.8 us
    unnamed x1, local copies, waits for them, and re-layouts  1.57 us

commit v1 on v0

--- a/solution.py
+++ b/solution.py
@@ -249,7 +249,7 @@
     payload = users // 2 + 2 * mine_t
     return pl.pallas_call(
         functools.partial(kernel, dims),
-        out_shape=jax.ShapeDtypeStruct(retained_branches.shape, f32),
+        out_shape=pltpu.VMEM(retained_branches.shape, f32),
         in_specs=[
             pl.BlockSpec(memory_space=pl.ANY),
             pl.BlockSpec(memory_space=pl.ANY),
@@ -272,7 +272,10 @@
         ],
         compiler_params=pltpu.CompilerParams(collective_id=0, has_side_effects=True),
         name="detect",
-    )(disturbance_variance.T, propagation_gains, observed_samples, retained_branches)
+    )(*(
+        pltpu.with_memory_space_constraint(x, pltpu.HBM)
+        for x in (disturbance_variance.T, propagation_gains, observed_samples, retained_branches)
+    ))
 
 
 def solution(mesh):

time: 20.6 us -> 19 us (0.922)
  local copies, waits for them, and re-layouts: 1.57 us -> 0.66 us
  Pallas kernels: 18.8 us -> 18.2 us
    unnamed x1, local copies, waits for them, and re-layouts: 1.57 us -> 0.66 us
    pallas_call x1, Pallas kernels: 18.8 us -> 18.2 us  [local(): pl.pallas_call(functools.partial(kernel, dims), out_shape=pltpu.VMEM(reta...]
where the time goes in v1:
time: 19 us; the launch traced here: 18.9 us
  Pallas kernels  18.2 us (96%)
  local copies, waits for them, and re-layouts  0.66 us (3%)
    pallas_call x1, Pallas kernels, local(): pl.pallas_call(functools.partial(kernel, dims), out_shape=pltpu.VMEM(reta...  18.2 us
    unnamed x1, local copies, waits for them, and re-layouts  0.66 us

profile of v1, /device:TPU:0, one launch (start us, length us, event | category | flops | bytes accessed | tf_op | source)
XLA Modules:
  0.0 18.9 jit_solution(12972193739389237852)
XLA Ops:
  0.0 18.2 %detect.1 = f32[4,2,4,1024]{3,2,1,0:T(4,128)S(1)} custom-call(f32[2,4]{1,0:T(2,128)} %bitcast.1, bf16[1,16,64,1024]{3,2,1,0:T(8,128)(2,1)} %gains_ref.1, bf16[1,16,32,1024]{3,2,1,0:T(8,128)(2,1)} %samples_ref.1, s32[4,2,4,1024]{3,2,1,0:T(4,128)} %branches_any.1), custom_call_target="tpu_custom_call" | custom-call | tf_op jit(solution)/shard_map/detect/pallas_call | solution.py:250
  18.2 0.7 %copy.6 = f32[4,2,4,1024]{3,2,1,0:T(4,128)} copy(f32[4,2,4,1024]{3,2,1,0:T(4,128)S(1)} %detect.1) | data formatting | bytes 262144

commit v2 on v1

--- a/solution.py
+++ b/solution.py
@@ -71,18 +71,17 @@
     for a in blocks:
         full = jnp.concatenate(a, axis=0)
         pivots = jnp.sum(jnp.where(lane == 2 * line, full, 0.0), axis=1, keepdims=True)
-        out.append(jnp.where(keep, full * lax.rsqrt(pivots), 0.0))
+        scale = jnp.where(lane < 2 * users, constellation_norm, 1.0)
+        out.append(jnp.where(keep, full * (lax.rsqrt(pivots) * scale), 0.0))
     return out
 
 
 def kernel(
     dims, noise_any, gains_ref, samples_ref, branches_any, out_ref,
-    noise_ref, branches_ref, held, raw, part, came, points, packed, taken, rotations,
+    noise_ref, branches_ref, held, raw, part, came, points, packed, taken,
     small_sem, load_sem, send_sem, recv_sem, usend_sem, urecv_sem,
 ):
     clusters, bands, users, symbols, share, mine_t, pieces = dims
-    copies = LANES // users
-    lines = pieces * mine_t
     me, band = lax.axis_index("chain"), lax.axis_index("par")
 
     barrier = pltpu.get_barrier_semaphore()
@@ -139,13 +138,31 @@
 
     for copy in small:
         copy.wait()
+    rows = pieces * mine_t
+    source, target = iota((2 * LANES, 4 * LANES), 0), iota((2 * LANES, 4 * LANES), 1)
+    place = target % (2 * LANES)
+    user, quadrature, off = place // 2, place % 2, target // (2 * LANES)
+    entry = jnp.where(source == user + LANES * ((quadrature + off) % 2), 1.0, 0.0)
+    entry = jnp.where(off * quadrature == 1, -entry, entry).astype(jnp.bfloat16)
+    marks = jnp.concatenate(
+        [
+            branches_ref[b, s, :, LANES * r : LANES * (r + 1)]
+            for b in range(bands) for s in range(share) for r in range(pieces)
+        ],
+        axis=0,
+    )
+    pair = jnp.concatenate(
+        [(2 * (marks & 7) - 7).astype(jnp.float32), (2 * (marks >> 3) - 7).astype(jnp.float32)], axis=1
+    ).astype(jnp.bfloat16)
+    woven = jnp.dot(pair, entry, preferred_element_type=jnp.float32).astype(jnp.bfloat16)
     for b in range(bands):
         for s in range(share):
-            q = jnp.concatenate(
-                [branches_ref[b, s, :, LANES * r : LANES * (r + 1)] for r in range(pieces)], axis=0
-            )
-            points[b, s, :, :LANES] = (2 * (q & 7) - 7).astype(jnp.float32).astype(jnp.bfloat16)
-            points[b, s, :, LANES:] = (2 * (q >> 3) - 7).astype(jnp.float32).astype(jnp.bfloat16)
+            first = (b * share + s) * rows
+            for h in range(2):
+                for o in range(2):
+                    points[b, s, pl.ds((2 * h + o) * rows, rows), :] = woven[
+                        first : first + rows, LANES * (2 * o + h) : LANES * (2 * o + h + 1)
+                    ]
 
     lane, line = iota((users, LANES), 1), iota((users, LANES), 0)
     noises = [
@@ -162,75 +179,78 @@
     ]
     factors = eliminate(mats, users)
 
-    source, target = iota((LANES, LANES), 0), iota((LANES, LANES), 1) % (2 * users)
-    spread = (source == 2 * (target % users) + target // users).astype(jnp.float32).astype(jnp.bfloat16)
-    rows = 2 * mine_t
-    r, c = iota((bands * rows, LANES), 0), iota((bands * rows, LANES), 1)
-    is_odd = (r % rows) // mine_t
-    wanted = 2 * users + 2 * ((r // rows) * mine_t + r % mine_t) + is_odd
-    pick = jnp.where(c == wanted, (1 - 2 * is_odd).astype(jnp.float32), 0.0).astype(jnp.bfloat16)
-    pick = jnp.concatenate([pick, pick], axis=1)
-    half = users // 2
-    left = iota((half, LANES), 1) < 2 * users
+    half, width, extra = users // 2, 2 * users, 2 * mine_t
+    spot = iota((half, LANES), 1)
     for s, factor in enumerate(factors):
-        high, low = split(factor * constellation_norm)
-        wide = jnp.dot(high, spread, preferred_element_type=jnp.float32) + jnp.dot(
-            low, spread, preferred_element_type=jnp.float32
-        )
-        folded = jnp.where(left, wide[:half], wide[half:])
-        for k in range(bands):
-            packed[k, s, :half] = folded
-        high, low = split(factor)
-        weights = jnp.concatenate(
-            [jnp.concatenate([high] * copies, axis=0), jnp.concatenate([low] * copies, axis=0)], axis=1
-        )
-        rotations[s] = lax.dot_general(pick, weights, NT, preferred_element_type=jnp.float32)
-        for k in range(bands):
-            peer = lax.rem(band + k, bands)
-            packed[k, s, half:] = rotations[s, pl.ds(pl.multiple_of(peer * rows, rows), rows), :]
+        top, bottom = factor[:half], factor[half:]
+        turned = pltpu.roll(bottom, width, 1)
+        for b in range(bands):
+            upper = pltpu.roll(top, LANES - extra * b, 1) if b else top
+            lower = pltpu.roll(bottom, (LANES + extra - extra * b) % LANES, 1) if b != 1 else bottom
+            packed[b, s] = jnp.where(
+                spot < width, top,
+                jnp.where(spot >= width + users, turned, jnp.where(spot < width + extra, upper, lower)),
+            )
+    near = []
+    inner = jnp.minimum(band, bands - 1 - band)
+    outward = jnp.where(2 * band < bands - 1, 1, -1)
+    for i in range(1, bands):
+        both_sides = (i + 1) // 2 if i % 2 else -(i // 2)
+        near.append(band + jnp.where(i <= 2 * inner, both_sides, outward * (i - inner)))
     usends = []
-    for k in range(1, bands):
+    for i in range(bands - 1, 0, -1):
+        peer = near[i - 1]
         copy = pltpu.make_async_remote_copy(
-            src_ref=packed.at[k], dst_ref=taken.at[k], send_sem=usend_sem.at[k], recv_sem=urecv_sem.at[k],
-            device_id={"par": lax.rem(band + k, bands)}, device_id_type=MESH,
+            src_ref=packed.at[peer], dst_ref=taken.at[band], send_sem=usend_sem.at[i], recv_sem=urecv_sem.at[band],
+            device_id={"par": peer}, device_id_type=MESH,
         )
         copy.start()
         usends.append(copy)
 
-    sr, sc = iota((LANES, LANES), 0), iota((LANES, LANES), 1)
-    suffix = jnp.where((sr // users == sc // users) & (sr >= sc), 1.0 / users, 0.0).astype(jnp.bfloat16)
-    suffix = jnp.concatenate([suffix, suffix], axis=0)
-    lane_block = lane // users
-    for k in range(bands):
-        if k:
-            usends[k - 1].wait_recv()
-        b = lax.rem(band + bands - k, bands)
-        box = taken if k else packed
+    r, c = iota((4 * rows, LANES), 0), iota((4 * rows, LANES), 1)
+    is_off = (r // rows) % 2
+    hit = ((c - width) % extra == 2 * (r % mine_t) + is_off) & (c >= width) & (c < width + 2 * extra)
+    chosen = jnp.where(hit, (2 * is_off - 1).astype(jnp.float32), 0.0).astype(jnp.bfloat16)
+    sr, sc = iota((width, LANES), 0), iota((width, LANES), 1)
+    suffix = [
+        jnp.where((sr // users + 2 * h == sc // users) & (sr % users >= sc % users), 1.0 / users, 0.0).astype(jnp.bfloat16)
+        for h in range(2)
+    ]
+    for i in range(bands):
+        b = band if i == 0 else near[i - 1]
+        if i:
+            pltpu.make_async_remote_copy(
+                src_ref=packed.at[b], dst_ref=taken.at[b], send_sem=usend_sem.at[i], recv_sem=urecv_sem.at[b],
+                device_id={"par": b}, device_id_type=MESH,
+            ).wait_recv()
+        box = taken if i else packed
         for s in range(share):
-            folded = box[k, s, :half]
-            crossed = pltpu.roll(folded, 2 * users, 1)
-            first = jnp.concatenate(
-                [jnp.where(left, folded, crossed), jnp.where(left, crossed, folded)], axis=0
-            )
-            second = pltpu.roll(first, users, 1)
-            ons, offs = [], []
-            for i in range(copies):
-                here = lane_block == i
-                real, imag = (first, second) if i % 2 == 0 else (second, first)
-                real, imag = jnp.where(here, real, 0.0), jnp.where(here, imag, 0.0)
-                ons.append(jnp.concatenate([real, imag], axis=1))
-                offs.append(jnp.concatenate([-imag, real], axis=1))
-            high, low = split(jnp.concatenate(ons + offs, axis=0))
-            p = points[b, s]
-            mapped = lax.dot_general(p, high, NT, preferred_element_type=jnp.float32) + lax.dot_general(
+            folded = box[b, s]
+            crossed = pltpu.roll(folded, width, 1)
+            weights = jnp.concatenate(
+                [
+                    jnp.where(spot < width, folded, 0.0),
+                    jnp.where((spot >= users) & (spot < width), crossed, 0.0),
+                    jnp.where(spot >= width, crossed, 0.0),
+                    jnp.where(spot >= width + users, folded, 0.0),
+                ],
+                axis=0,
+            )
+            own = [
+                jnp.where((spot >= width) & (spot < width + extra), folded, 0.0),
+                jnp.where((spot >= width + extra) & (spot < width + 2 * extra), folded, 0.0),
+            ]
+            high, low = split(jnp.concatenate([weights, jnp.concatenate(own + own, axis=0)], axis=1))
+            p = jnp.concatenate([points[b, s], chosen], axis=1)
+            rest = lax.dot_general(p, high, NT, preferred_element_type=jnp.float32) + lax.dot_general(
                 p, low, NT, preferred_element_type=jnp.float32
             )
-            on = jnp.concatenate([box[k, s, half : half + mine_t]] * pieces, axis=0) - mapped[:, :LANES]
-            off = jnp.concatenate([box[k, s, half + mine_t :]] * pieces, axis=0) - mapped[:, LANES:]
-            high, low = split(on * on + off * off)
-            result = jnp.dot(
-                jnp.concatenate([high, low], axis=1), suffix, preferred_element_type=jnp.float32
-            )
+            result = None
+            for h in range(2):
+                on, off = rest[2 * h * rows : (2 * h + 1) * rows], rest[(2 * h + 1) * rows : (2 * h + 2) * rows]
+                for term in split(on * on + off * off):
+                    step = jnp.dot(term, suffix[h], preferred_element_type=jnp.float32)
+                    result = step if result is None else result + step
             for r in range(pieces):
                 out_ref[b, s, :, LANES * r : LANES * (r + 1)] = result[mine_t * r : mine_t * (r + 1)]
     for copy in sends + usends:
@@ -246,7 +266,7 @@
     dims = (clusters, bands, users, symbols, share, mine_t, pieces)
     f32, bf16 = jnp.float32, jnp.bfloat16
     vmem, dma = pltpu.VMEM, pltpu.SemaphoreType.DMA
-    payload = users // 2 + 2 * mine_t
+    payload = users // 2
     return pl.pallas_call(
         functools.partial(kernel, dims),
         out_shape=pltpu.VMEM(retained_branches.shape, f32),
@@ -264,10 +284,9 @@
             vmem((4, 2 * users, LANES), f32),
             vmem((clusters, share, users, LANES), f32),
             vmem((clusters, share, users, LANES), f32),
-            vmem((bands, share, pieces * mine_t, 2 * LANES), bf16),
+            vmem((bands, share, 4 * pieces * mine_t, LANES), bf16),
             vmem((bands, share, payload, LANES), f32),
             vmem((bands, share, payload, LANES), f32),
-            vmem((share, bands * 2 * mine_t, LANES), f32),
             dma((2,)), dma((2, clusters)), dma((clusters,)), dma((clusters,)), dma((bands,)), dma((bands,)),
         ],
         compiler_params=pltpu.CompilerParams(collective_id=0, has_side_effects=True),

time: 19 us -> 17.1 us (0.900)
  Pallas kernels: 18.2 us -> 16.2 us
    pallas_call x1, Pallas kernels: 18.2 us -> 16.2 us  [local(): pl.pallas_call(functools.partial(kernel, dims), out_shape=pltpu.VMEM(reta...]
where the time goes in v2:
time: 17.1 us; the launch traced here: 16.9 us
  Pallas kernels  16.2 us (95%)
  local copies, waits for them, and re-layouts  0.66 us (4%)
    pallas_call x1, Pallas kernels, local(): pl.pallas_call(functools.partial(kernel, dims), out_shape=pltpu.VMEM(reta...  16.2 us
    unnamed x1, local copies, waits for them, and re-layouts  0.66 us

profile of v2, /device:TPU:0, one launch (start us, length us, event | category | flops | bytes accessed | tf_op | source)
XLA Modules:
  0.0 16.9 jit_solution(15441778981965873577)
XLA Ops:
  0.0 16.2 %detect.1 = f32[4,2,4,1024]{3,2,1,0:T(4,128)S(1)} custom-call(f32[2,4]{1,0:T(2,128)} %bitcast.1, bf16[1,16,64,1024]{3,2,1,0:T(8,128)(2,1)} %gains_ref.1, bf16[1,16,32,1024]{3,2,1,0:T(8,128)(2,1)} %samples_ref.1, s32[4,2,4,1024]{3,2,1,0:T(4,128)} %branches_any.1), custom_call_target="tpu_custom_call" | custom-call | tf_op jit(solution)/shard_map/detect/pallas_call | solution.py:270
  16.3 0.7 %copy.6 = f32[4,2,4,1024]{3,2,1,0:T(4,128)} copy(f32[4,2,4,1024]{3,2,1,0:T(4,128)S(1)} %detect.1) | data formatting | bytes 262144

commit v3 on v2

--- a/solution.py
+++ b/solution.py
@@ -35,16 +35,25 @@
         parts = [mat[8 * g : 8 * g + 8, :] for g in range(groups)]
         blocks.append(parts)
         turned.append([jnp.where(odd, pair_swap(p), -pair_swap(p)) for p in parts])
-    row = iota((8, LANES), 0)
+    row, lanes = iota((8, LANES), 0), iota((8, LANES), 1)
     for start in range(0, users, PANEL):
         home = start // 8
-        panels = [
-            [
-                {g: jnp.broadcast_to(a[g][:, lane : lane + 1], (8, LANES)) for g in range(home, groups)}
-                for lane in range(2 * start, 2 * (start + PANEL))
-            ]
-            for a in blocks
-        ]
+        panels = []
+        for a in blocks:
+            panel = []
+            for j in range(start, start + PANEL):
+                pivot = jnp.broadcast_to(a[home][j % 8 : j % 8 + 1, :], (8, LANES)) if start < users // 2 else None
+                for part in range(2):
+                    column = {}
+                    for g in range(home, groups):
+                        if start < users // 2 <= 8 * g:
+                            found = jnp.where(lanes == 2 * (row + 8 * g) + part, pivot, 0.0)
+                            found = jnp.sum(-found if part else found, axis=1, keepdims=True)
+                        else:
+                            found = a[g][:, 2 * j + part : 2 * j + part + 1]
+                        column[g] = jnp.broadcast_to(found, (8, LANES))
+                    panel.append(column)
+            panels.append(panel)
         for j in range(start, min(start + PANEL, users - 1)):
             at, c = j % 8, j - start
             for a, ia, panel in zip(blocks, turned, panels):
@@ -81,7 +90,7 @@
     noise_ref, branches_ref, held, raw, part, came, points, packed, taken,
     small_sem, load_sem, send_sem, recv_sem, usend_sem, urecv_sem,
 ):
-    clusters, bands, users, symbols, share, mine_t, pieces = dims
+    clusters, bands, users, symbols, share, mine_t, pieces, compact = dims
     me, band = lax.axis_index("chain"), lax.axis_index("par")
 
     barrier = pltpu.get_barrier_semaphore()
@@ -90,10 +99,17 @@
     for k in range(1, bands):
         pl.semaphore_signal(barrier, inc=1, device_id={"par": lax.rem(band + k, bands)}, device_id_type=MESH)
 
-    order = list(range(1, clusters)) + [0]
+    order = list(range(clusters - 1, -1, -1))
+    peers = {}
+    for k in order:
+        peers[k], bit = me - me, 1
+        while bit < clusters:
+            digit = lax.rem(me // bit, 2)
+            peers[k] = peers[k] + bit * (1 - digit if (k // bit) % 2 else digit)
+            bit *= 2
     loads = {}
     for k in order:
-        tones = pl.ds(lax.rem(me + k, clusters) * share, share)
+        tones = pl.ds(peers[k] * share, share)
         loads[k] = (
             pltpu.make_async_copy(
                 gains_ref.at[0, tones], held.at[k, :, pl.ds(0, 2 * users)], load_sem.at[0, k]
@@ -112,29 +128,54 @@
     for copy in small:
         copy.start()
     raw[...] = jnp.zeros_like(raw)
-    even = iota((users, LANES), 1) % 2 == 0
+    half, width = users // 2, 2 * users
+    even, at = iota((users, LANES), 1) % 2 == 0, iota((half, LANES), 1)
+    at8 = iota((8, LANES), 1) // users
     sends = []
-    for number, k in enumerate(order):
-        for copy in loads[k]:
-            copy.wait()
-        for s in range(share):
+
+    def fold(number, k, products):
+        tiles = []
+        for s, product in enumerate(products):
             slot = (number * share + s) % raw.shape[0]
-            both = held[k, s]
-            raw[slot, :, : 2 * (users + symbols)] = lax.dot_general(
-                both[: 2 * users], both, NT, preferred_element_type=jnp.float32
-            )
+            raw[slot, :, : width + 2 * symbols] = product
             on_even = raw[slot, pl.ds(0, users, stride=2), :]
             on_odd = raw[slot, pl.ds(1, users, stride=2), :]
-            part[k, s] = pair_swap(on_odd) + jnp.where(even, on_even, -on_even)
+            whole = pair_swap(on_odd) + jnp.where(even, on_even, -on_even)
+            if not compact:
+                part[k, s * users : (s + 1) * users] = whole
+                continue
+            lower = whole[half:]
+            moved = pltpu.roll(lower, users, 1)
+            part[k, s * half : (s + 1) * half] = jnp.where(at < 3 * users, whole[:half], moved)
+            tiles.append((lower[:8], lower[8:], moved[:8]))
+        if compact:
+            (first, second, turned), (third, fourth, _) = tiles
+            part[k, share * half :] = jnp.where(
+                at8 == 0, pltpu.roll(third, LANES - users, 1),
+                jnp.where(at8 == 1, second, jnp.where(at8 == 2, turned, pltpu.roll(fourth, 2 * users, 1))),
+            )
         if k:
             if number == 0:
                 pl.semaphore_wait(barrier, clusters + bands - 2)
             copy = pltpu.make_async_remote_copy(
                 src_ref=part.at[k], dst_ref=came.at[k], send_sem=send_sem.at[k], recv_sem=recv_sem.at[k],
-                device_id={"chain": lax.rem(me + k, clusters)}, device_id_type=MESH,
+                device_id={"chain": peers[k]}, device_id_type=MESH,
             )
             copy.start()
             sends.append(copy)
+
+    waiting = None
+    for number, k in enumerate(order):
+        for copy in loads[k]:
+            copy.wait()
+        products = []
+        for s in range(share):
+            both = held[k, s]
+            products.append(lax.dot_general(both[:width], both, NT, preferred_element_type=jnp.float32))
+        if waiting:
+            fold(*waiting)
+        waiting = (number, k, products)
+    fold(*waiting)
 
     for copy in small:
         copy.wait()
@@ -169,18 +210,29 @@
         jnp.sum(jnp.where(iota((1, bands), 1) == band, noise_ref[s : s + 1, :], 0.0), axis=1, keepdims=True)
         for s in range(share)
     ]
-    totals = [part[0, s] for s in range(share)]
     for copy in sends:
         copy.wait_recv()
+    total = part[0]
     for k in range(1, clusters):
-        totals = [total + came[k, s] for s, total in enumerate(totals)]
-    mats = [
-        jnp.where(lane == 2 * line, total + noises[s], total) for s, total in enumerate(totals)
-    ]
+        total = total + came[k]
+    if compact:
+        tile, mats = total[share * half :], []
+        for s in range(share):
+            upper = total[s * half : (s + 1) * half]
+            back = pltpu.roll(upper, LANES - users, 1)
+            corner = jnp.concatenate(
+                [pltpu.roll(tile, LANES - users, 1), tile] if s == 0
+                else [pltpu.roll(tile, users, 1), pltpu.roll(tile, 2 * users, 1)],
+                axis=0,
+            )
+            lower = jnp.where((at >= users) & (at < width), corner, jnp.where((at >= width) & (at < 3 * users), back, 0.0))
+            mats.append(jnp.concatenate([jnp.where(at < 3 * users, upper, 0.0), lower], axis=0))
+    else:
+        mats = [total[s * users : (s + 1) * users] for s in range(share)]
+    mats = [jnp.where(lane == 2 * line, mat + noises[s], mat) for s, mat in enumerate(mats)]
     factors = eliminate(mats, users)
 
-    half, width, extra = users // 2, 2 * users, 2 * mine_t
-    spot = iota((half, LANES), 1)
+    extra, spot = 2 * mine_t, at
     for s, factor in enumerate(factors):
         top, bottom = factor[:half], factor[half:]
         turned = pltpu.roll(bottom, width, 1)
@@ -263,7 +315,9 @@
     users, symbols = double_users // 2, observed_samples.shape[2] // 2
     share, mine_t = tones // clusters, symbols // bands
     pieces = retained_branches.shape[-1] // LANES
-    dims = (clusters, bands, users, symbols, share, mine_t, pieces)
+    compact = share == 2 and users == 32 and 2 * symbols <= users
+    lines = share * users // 2 + 8 if compact else share * users
+    dims = (clusters, bands, users, symbols, share, mine_t, pieces, compact)
     f32, bf16 = jnp.float32, jnp.bfloat16
     vmem, dma = pltpu.VMEM, pltpu.SemaphoreType.DMA
     payload = users // 2
@@ -282,8 +336,8 @@
             vmem(retained_branches.shape, jnp.int32),
             vmem((clusters, share, 2 * (users + symbols), antennas), bf16),
             vmem((4, 2 * users, LANES), f32),
-            vmem((clusters, share, users, LANES), f32),
-            vmem((clusters, share, users, LANES), f32),
+            vmem((clusters, lines, LANES), f32),
+            vmem((clusters, lines, LANES), f32),
             vmem((bands, share, 4 * pieces * mine_t, LANES), bf16),
             vmem((bands, share, payload, LANES), f32),
             vmem((bands, share, payload, LANES), f32),

time: 17.1 us -> 16.9 us (0.988)
  no operation moved by 1% of the time
where the time goes in v3:
time: 16.9 us; the launch traced here: 16.8 us
  Pallas kernels  16.1 us (95%)
  local copies, waits for them, and re-layouts  0.66 us (4%)
    pallas_call x1, Pallas kernels, local(): pl.pallas_call(functools.partial(kernel, dims), out_shape=pltpu.VMEM(reta...  16.1 us
    unnamed x1, local copies, waits for them, and re-layouts  0.66 us

profile of v3, /device:TPU:0, one launch (start us, length us, event | category | flops | bytes accessed | tf_op | source)
XLA Modules:
  0.0 16.8 jit_solution(5539764861016439915)
XLA Ops:
  0.0 16.1 %detect.1 = f32[4,2,4,1024]{3,2,1,0:T(4,128)S(1)} custom-call(f32[2,4]{1,0:T(2,128)} %bitcast.1, bf16[1,16,64,1024]{3,2,1,0:T(8,128)(2,1)} %gains_ref.1, bf16[1,16,32,1024]{3,2,1,0:T(8,128)(2,1)} %samples_ref.1, s32[4,2,4,1024]{3,2,1,0:T(4,128)} %branches_any.1), custom_call_target="tpu_custom_call" | custom-call | tf_op jit(solution)/shard_map/detect/pallas_call | solution.py:324
  16.1 0.7 %copy.6 = f32[4,2,4,1024]{3,2,1,0:T(4,128)} copy(f32[4,2,4,1024]{3,2,1,0:T(4,128)S(1)} %detect.1) | data formatting | bytes 262144

commit v4 on v2

v4 whole, which is shorter than its diff:
```python
import functools
import jax
import jax.numpy as jnp
from jax import lax
from jax.experimental import pallas as pl
from jax.experimental.pallas import tpu as pltpu
from jax.sharding import PartitionSpec as P

constellation_norm = 1.0 / 42.0**0.5
LANES = 128
MESH = pl.DeviceIdType.MESH
NT = (((1,), (1,)), ((), ()))


def iota(shape, dim):
    return lax.broadcasted_iota(jnp.int32, shape, dim)


def panels(users):
    wide = users // 2
    return [(j, 4) for j in range(0, wide, 4)] + [(j, 8) for j in range(wide, users, 8)]


def split(x):
    high = x.astype(jnp.bfloat16)
    return high, (x - high.astype(jnp.float32)).astype(jnp.bfloat16)


def pair_swap(x):
    even = iota(x.shape, 1) % 2 == 0
    return jnp.where(even, pltpu.roll(x, LANES - 1, 1), pltpu.roll(x, 1, 1))


def eliminate(lines, users):
    groups, width = users // 8, 2 * users
    row, lanes = iota((8, LANES), 0), iota((8, LANES), 1)
    spot, second = lanes % width, lanes >= width
    a = list(lines)
    ia = [jnp.where(lanes % 2 == 1, pair_swap(p), -pair_swap(p)) for p in a[:groups]]
    by_row = [jnp.ones((8, LANES), jnp.float32) for _ in range(groups)]
    by_lane = jnp.ones((8, LANES), jnp.float32)

    def column(x, at):
        return jnp.where(second, x[:, width + at : width + at + 1], x[:, at : at + 1])

    for start, size in panels(users):
        home = start // 8
        panel = []
        for j in range(start, start + size):
            pivot = jnp.broadcast_to(a[home][j % 8 : j % 8 + 1, :], (8, LANES))
            for c in range(2):
                found = {}
                for g in range(home, len(a)):
                    if start < users // 2 <= 8 * g < users:
                        ones = [
                            jnp.sum(jnp.where(lanes == t * width + 2 * (row + 8 * g) + c, pivot, 0.0), axis=1, keepdims=True)
                            for t in range(2)
                        ]
                        found[g] = jnp.where(second, ones[1], ones[0])
                        if c:
                            found[g] = -found[g]
                    else:
                        found[g] = column(a[g], 2 * j + c)
                panel.append(found)
        for j in range(start, start + size):
            at, c = j % 8, j - start
            real, imag = panel[2 * c], panel[2 * c + 1]
            top = real[home][at : at + 1, :]
            root, inverse = lax.rsqrt(top), 1.0 / top
            by_row[home] = jnp.where(row == at, root, by_row[home])
            by_lane = jnp.where(spot // 2 == j, root, by_lane)
            beyond = spot[:1] > 2 * j + 1
            pivot_row = jnp.where(beyond, a[home][at : at + 1, :] * inverse, 0.0)
            turned_row = jnp.where(beyond, ia[home][at : at + 1, :] * inverse, 0.0)
            later = [
                (d, real[home][at + d - c : at + d - c + 1, :] * inverse, imag[home][at + d - c : at + d - c + 1, :] * inverse)
                for d in range(c + 1, size)
            ]
            for g in range(home, len(a)):
                if g == home and at == 7:
                    continue
                fr, fi = real[g], imag[g]
                if g == home:
                    fr, fi = jnp.where(row > at, fr, 0.0), jnp.where(row > at, fi, 0.0)
                for d, x, y in later:
                    panel[2 * d][g] = panel[2 * d][g] - (fr * x + fi * y)
                    panel[2 * d + 1][g] = panel[2 * d + 1][g] - (fi * x - fr * y)
                if j < users - 1:
                    a[g] = a[g] - (fr * pivot_row + fi * turned_row)
                    if g < groups:
                        ia[g] = ia[g] - (fr * turned_row - fi * pivot_row)
    upper = []
    for g in range(groups):
        diagonal = 2 * (row + 8 * g)
        keep = (spot >= diagonal) & (spot != diagonal + 1)
        upper.append(jnp.where(keep, a[g] * (by_row[g] * constellation_norm), 0.0))
    return upper, [x * by_lane for x in a[groups:]]


def kernel(
    dims, noise_any, gains_ref, samples_ref, branches_any, out_ref,
    noise_ref, branches_ref, held, raw, part, came, points, packed, taken,
    small_sem, load_sem, send_sem, recv_sem, usend_sem, urecv_sem,
):
    clusters, bands, users, symbols, share, mine_t, pieces = dims
    me, band = lax.axis_index("chain"), lax.axis_index("par")

    barrier = pltpu.get_barrier_semaphore()
    for k in range(1, clusters):
        pl.semaphore_signal(barrier, inc=1, device_id={"chain": lax.rem(me + k, clusters)}, device_id_type=MESH)
    for k in range(1, bands):
        pl.semaphore_signal(barrier, inc=1, device_id={"par": lax.rem(band + k, bands)}, device_id_type=MESH)

    order = list(range(clusters - 1, -1, -1))
    peers = {}
    for k in order:
        peers[k], bit = me - me, 1
        while bit < clusters:
            digit = lax.rem(me // bit, 2)
            peers[k] = peers[k] + bit * (1 - digit if (k // bit) % 2 else digit)
            bit *= 2
    loads = {}
    for k in order:
        tones = pl.ds(peers[k] * share, share)
        loads[k] = (
            pltpu.make_async_copy(
                gains_ref.at[0, tones], held.at[k, :, pl.ds(0, 2 * users)], load_sem.at[0, k]
            ),
            pltpu.make_async_copy(
                samples_ref.at[0, tones], held.at[k, :, pl.ds(2 * users, 2 * symbols)], load_sem.at[1, k]
            ),
        )
        for copy in loads[k]:
            copy.start()

    small = (
        pltpu.make_async_copy(noise_any, noise_ref, small_sem.at[0]),
        pltpu.make_async_copy(branches_any, branches_ref, small_sem.at[1]),
    )
    for copy in small:
        copy.start()
    half, quarter, width, depth = users // 2, users // 4, 2 * users, 2 * (users + symbols)
    sends = []

    def fold(number, k, product):
        slot = number % raw.shape[0]
        raw[slot] = jnp.where(iota((depth, LANES), 1) < width, product[:depth], product[depth:])
        on_even = raw[slot, pl.ds(0, depth // 2, stride=2), :]
        on_odd = raw[slot, pl.ds(1, depth // 2, stride=2), :]
        even = iota((depth // 2, LANES), 1) % 2 == 0
        whole = pair_swap(on_odd) + jnp.where(even, on_even, -on_even)
        part[k, :half] = whole[:half]
        part[k, half : half + quarter] = jnp.where(
            iota((quarter, LANES), 1) % width >= users,
            whole[half + quarter : users],
            pltpu.roll(whole[half : half + quarter], LANES - users, 1),
        )
        part[k, half + quarter :] = whole[users:]
        if k:
            if number == 0:
                pl.semaphore_wait(barrier, clusters + bands - 2)
            copy = pltpu.make_async_remote_copy(
                src_ref=part.at[k], dst_ref=came.at[k], send_sem=send_sem.at[k], recv_sem=recv_sem.at[k],
                device_id={"chain": peers[k]}, device_id_type=MESH,
            )
            copy.start()
            sends.append(copy)

    waiting = None
    for number, k in enumerate(order):
        for copy in loads[k]:
            copy.wait()
        fixed = jnp.concatenate([held[k, s, :width] for s in range(share)], axis=0)
        streamed = jnp.concatenate([held[k, s] for s in range(share)], axis=0)
        product = lax.dot_general(streamed, fixed, NT, preferred_element_type=jnp.float32)
        if waiting:
            fold(*waiting)
        waiting = (number, k, product)
    fold(*waiting)

    for copy in small:
        copy.wait()
    rows = pieces * mine_t
    source, target = iota((2 * LANES, 4 * LANES), 0), iota((2 * LANES, 4 * LANES), 1)
    place = target % (2 * LANES)
    user, quadrature, off = place // 2, place % 2, target // (2 * LANES)
    entry = jnp.where(source == user + LANES * ((quadrature + off) % 2), 1.0, 0.0)
    entry = jnp.where(off * quadrature == 1, -entry, entry).astype(jnp.bfloat16)
    marks = jnp.concatenate(
        [
            branches_ref[b, s, :, LANES * r : LANES * (r + 1)]
            for b in range(bands) for s in range(share) for r in range(pieces)
        ],
        axis=0,
    )
    pair = jnp.concatenate(
        [(2 * (marks & 7) - 7).astype(jnp.float32), (2 * (marks >> 3) - 7).astype(jnp.float32)], axis=1
    ).astype(jnp.bfloat16)
    woven = jnp.dot(pair, entry, preferred_element_type=jnp.float32).astype(jnp.bfloat16)
    for b in range(bands):
        for s in range(share):
            first = (b * share + s) * rows
            for h in range(2):
                for o in range(2):
                    points[b, s, pl.ds((2 * h + o) * rows, rows), :] = woven[
                        first : first + rows, LANES * (2 * o + h) : LANES * (2 * o + h + 1)
                    ]

    noises = [
        jnp.sum(jnp.where(iota((1, bands), 1) == band, noise_ref[s : s + 1, :], 0.0), axis=1, keepdims=True)
        for s in range(share)
    ]
    row, lanes = iota((8, LANES), 0), iota((8, LANES), 1)
    noise = jnp.where(lanes >= width, noises[1], noises[0])
    for copy in sends:
        copy.wait_recv()
    total = part[0]
    for k in range(1, clusters):
        total = total + came[k]
    corner = total[half : half + quarter]
    inside = iota((quarter, LANES), 1) % width >= users
    lower = [jnp.where(inside, x, 0.0) for x in (pltpu.roll(corner, users, 1), corner)]
    mats = jnp.concatenate([total[:half]] + lower + [total[half + quarter :]], axis=0)
    lines = [mats[8 * g : 8 * g + 8] for g in range((users + symbols) // 8)]
    for g in range(users // 8):
        lines[g] = jnp.where(lanes % width == 2 * (row + 8 * g), lines[g] + noise, lines[g])
    upper, rotated = eliminate(lines, users)
    upper, rotated = jnp.concatenate(upper, axis=0), jnp.concatenate(rotated, axis=0)
    corner = jnp.where(inside, upper[half + quarter :], pltpu.roll(upper[half : half + quarter], LANES - users, 1))
    for b in range(bands):
        packed[b, :half] = upper[:half]
        packed[b, half : half + quarter] = corner
        packed[b, half + quarter :] = rotated[mine_t * b : mine_t * (b + 1)]
    near = []
    inner = jnp.minimum(band, bands - 1 - band)
    outward = jnp.where(2 * band < bands - 1, 1, -1)
    for i in range(1, bands):
        both_sides = (i + 1) // 2 if i % 2 else -(i // 2)
        near.append(band + jnp.where(i <= 2 * inner, both_sides, outward * (i - inner)))
    usends = []
    for i in range(bands - 1, 0, -1):
        peer = near[i - 1]
        copy = pltpu.make_async_remote_copy(
            src_ref=packed.at[peer], dst_ref=taken.at[band], send_sem=usend_sem.at[i], recv_sem=urecv_sem.at[band],
            device_id={"par": peer}, device_id_type=MESH,
        )
        copy.start()
        usends.append(copy)

    r, c = iota((width, LANES), 0), iota((width, LANES), 1)
    minus = jnp.where(c % width // 2 == r % users, -1.0, 0.0).astype(jnp.bfloat16)
    sr, sc = iota((width, LANES), 0), iota((width, LANES), 1)
    suffix = [
        jnp.where((sr // users + 2 * h == sc // users) & (sr % users >= sc % users), 1.0 / users, 0.0).astype(jnp.bfloat16)
        for h in range(2)
    ]
    for i in range(bands):
        b = band if i == 0 else near[i - 1]
        if i:
            pltpu.make_async_remote_copy(
                src_ref=packed.at[b], dst_ref=taken.at[b], send_sem=usend_sem.at[i], recv_sem=urecv_sem.at[b],
                device_id={"par": b}, device_id_type=MESH,
            ).wait_recv()
        box = taken if i else packed
        top, corner = box[b, :half], box[b, half : half + quarter]
        straight = [(top, corner, pltpu.roll(corner, users, 1))]
        straight.append((pltpu.roll(top, width, 1), pltpu.roll(corner, width, 1), pltpu.roll(corner, 3 * users, 1)))
        z = box[b, half + quarter :]
        low = pltpu.roll(z, width, 1)
        low = low - low.astype(jnp.bfloat16).astype(jnp.float32)
        side, edge = iota(top.shape, 1) // width, iota(corner.shape, 1) // users
        for s in range(share):
            weights = []
            for e in range(2):
                above, fourth, third = straight[(s + e) % 2]
                weights += [
                    jnp.where(side == e, above, 0.0),
                    jnp.where(edge == 2 * e + 1, third, 0.0),
                    jnp.where(edge == 2 * e + 1, fourth, 0.0),
                ]
            high, rest_of = split(jnp.concatenate(weights, axis=0))
            zl = iota(z.shape, 1)
            both = jnp.where(zl // width == s, z, low)
            both = jnp.concatenate(
                [jnp.concatenate([jnp.where(zl % 2 == o, both, 0.0)] * pieces, axis=0) for o in range(2)] * 2, axis=0
            ).astype(jnp.bfloat16)
            p = points[b, s]
            rest = lax.dot_general(
                jnp.concatenate([p, both], axis=1), jnp.concatenate([high, minus], axis=1), NT,
                preferred_element_type=jnp.float32,
            ) + lax.dot_general(p, rest_of, NT, preferred_element_type=jnp.float32)
            result = None
            for h in range(2):
                on, off = rest[2 * h * rows : (2 * h + 1) * rows], rest[(2 * h + 1) * rows : (2 * h + 2) * rows]
                for term in split(on * on + off * off):
                    step = jnp.dot(term, suffix[h], preferred_element_type=jnp.float32)
                    result = step if result is None else result + step
            for r in range(pieces):
                out_ref[b, s, :, LANES * r : LANES * (r + 1)] = result[mine_t * r : mine_t * (r + 1)]
    for copy in sends + usends:
        copy.wait_send()


def local(propagation_gains, observed_samples, disturbance_variance, retained_branches):
    clusters, bands = lax.axis_size("chain"), lax.axis_size("par")
    _, tones, double_users, antennas = propagation_gains.shape
    users, symbols = double_users // 2, observed_samples.shape[2] // 2
    share, mine_t = tones // clusters, symbols // bands
    pieces = retained_branches.shape[-1] // LANES
    assert share == 2 and 4 * users == LANES
    dims = (clusters, bands, users, symbols, share, mine_t, pieces)
    lines = 3 * users // 4
    f32, bf16 = jnp.float32, jnp.bfloat16
    vmem, dma = pltpu.VMEM, pltpu.SemaphoreType.DMA
    return pl.pallas_call(
        functools.partial(kernel, dims),
        out_shape=pltpu.VMEM(retained_branches.shape, f32),
        in_specs=[
            pl.BlockSpec(memory_space=pl.ANY),
            pl.BlockSpec(memory_space=pl.ANY),
            pl.BlockSpec(memory_space=pl.ANY),
            pl.BlockSpec(memory_space=pl.ANY),
        ],
        out_specs=pl.BlockSpec(memory_space=pltpu.VMEM),
        scratch_shapes=[
            vmem(disturbance_variance.shape[::-1], f32),
            vmem(retained_branches.shape, jnp.int32),
            vmem((clusters, share, 2 * (users + symbols), antennas), bf16),
            vmem((2, 2 * (users + symbols), LANES), f32),
            vmem((clusters, lines + symbols, LANES), f32),
            vmem((clusters, lines + symbols, LANES), f32),
            vmem((bands, share, 4 * pieces * mine_t, LANES), bf16),
            vmem((bands, lines + mine_t, LANES), f32),
            vmem((bands, lines + mine_t, LANES), f32),
            dma((2,)), dma((2, clusters)), dma((clusters,)), dma((clusters,)), dma((bands,)), dma((bands,)),
        ],
        compiler_params=pltpu.CompilerParams(collective_id=0, has_side_effects=True),
        name="detect",
    )(*(
        pltpu.with_memory_space_constraint(x, pltpu.HBM)
        for x in (disturbance_variance.T, propagation_gains, observed_samples, retained_branches)
    ))


def solution(mesh):
    placed = (
        P("par", None, None, "chain"),
        P("par", None, None, "chain"),
        P(None, "chain"),
        P(None, "chain", "par", None),
    )
    return jax.shard_map(
        local, mesh=mesh, in_specs=placed, out_specs=P(None, "chain", "par", None), check_vma=False
    )
```

time: 17.1 us -> 17.1 us (level)
  no operation moved by 1% of the time
where the time goes in v4:
time: 17.1 us; the launch traced here: 17 us
  Pallas kernels  16.3 us (95%)
  local copies, waits for them, and re-layouts  0.66 us (4%)
    pallas_call x1, Pallas kernels, local(): pl.pallas_call(functools.partial(kernel, dims), out_shape=pltpu.VMEM(reta...  16.3 us
    unnamed x1, local copies, waits for them, and re-layouts  0.66 us

profile of v4, /device:TPU:0, one launch (start us, length us, event | category | flops | bytes accessed | tf_op | source)
XLA Modules:
  0.0 17.0 jit_solution(4869394831140622385)
XLA Ops:
  0.0 16.3 %detect.1 = f32[4,2,4,1024]{3,2,1,0:T(4,128)S(1)} custom-call(f32[2,4]{1,0:T(2,128)} %bitcast.1, bf16[1,16,64,1024]{3,2,1,0:T(8,128)(2,1)} %gains_ref.1, bf16[1,16,32,1024]{3,2,1,0:T(8,128)(2,1)} %samples_ref.1, s32[4,2,4,1024]{3,2,1,0:T(4,128)} %branches_any.1), custom_call_target="tpu_custom_call" | custom-call | tf_op jit(solution)/shard_map/detect/pallas_call | solution.py:315
  16.3 0.7 %copy.6 = f32[4,2,4,1024]{3,2,1,0:T(4,128)} copy(f32[4,2,4,1024]{3,2,1,0:T(4,128)S(1)} %detect.1) | data formatting | bytes 262144

commit v5 on v4

--- a/solution.py
+++ b/solution.py
@@ -31,18 +31,12 @@
     return jnp.where(even, pltpu.roll(x, LANES - 1, 1), pltpu.roll(x, 1, 1))
 
 
-def eliminate(lines, users):
+def eliminate(a, q, users):
     groups, width = users // 8, 2 * users
     row, lanes = iota((8, LANES), 0), iota((8, LANES), 1)
-    spot, second = lanes % width, lanes >= width
-    a = list(lines)
-    ia = [jnp.where(lanes % 2 == 1, pair_swap(p), -pair_swap(p)) for p in a[:groups]]
+    tone = jnp.where(lanes >= width, width, 0)
+    ia, iq = [[jnp.where(lanes % 2 == 1, pair_swap(p), -pair_swap(p)) for p in x] for x in (a, q)]
     by_row = [jnp.ones((8, LANES), jnp.float32) for _ in range(groups)]
-    by_lane = jnp.ones((8, LANES), jnp.float32)
-
-    def column(x, at):
-        return jnp.where(second, x[:, width + at : width + at + 1], x[:, at : at + 1])
-
     for start, size in panels(users):
         home = start // 8
         panel = []
@@ -50,51 +44,47 @@
             pivot = jnp.broadcast_to(a[home][j % 8 : j % 8 + 1, :], (8, LANES))
             for c in range(2):
                 found = {}
-                for g in range(home, len(a)):
-                    if start < users // 2 <= 8 * g < users:
+                for g in range(home, groups):
+                    if start < users // 2 <= 8 * g:
                         ones = [
                             jnp.sum(jnp.where(lanes == t * width + 2 * (row + 8 * g) + c, pivot, 0.0), axis=1, keepdims=True)
                             for t in range(2)
                         ]
-                        found[g] = jnp.where(second, ones[1], ones[0])
+                        found[g] = jnp.where(lanes >= width, ones[1], ones[0])
                         if c:
                             found[g] = -found[g]
                     else:
-                        found[g] = column(a[g], 2 * j + c)
+                        found[g] = jnp.take_along_axis(a[g], tone + (2 * j + c), axis=1, mode="promise_in_bounds")
                 panel.append(found)
         for j in range(start, start + size):
             at, c = j % 8, j - start
             real, imag = panel[2 * c], panel[2 * c + 1]
             top = real[home][at : at + 1, :]
-            root, inverse = lax.rsqrt(top), 1.0 / top
-            by_row[home] = jnp.where(row == at, root, by_row[home])
-            by_lane = jnp.where(spot // 2 == j, root, by_lane)
-            beyond = spot[:1] > 2 * j + 1
-            pivot_row = jnp.where(beyond, a[home][at : at + 1, :] * inverse, 0.0)
-            turned_row = jnp.where(beyond, ia[home][at : at + 1, :] * inverse, 0.0)
+            by_row[home] = jnp.where(row == at, lax.rsqrt(top), by_row[home])
+            if j == users - 1:
+                break
+            inverse = 1.0 / top
+            pivots = [(x, ix, x[home][at : at + 1, :] * inverse, ix[home][at : at + 1, :] * inverse) for x, ix in ((a, ia), (q, iq))]
             later = [
                 (d, real[home][at + d - c : at + d - c + 1, :] * inverse, imag[home][at + d - c : at + d - c + 1, :] * inverse)
                 for d in range(c + 1, size)
             ]
-            for g in range(home, len(a)):
-                if g == home and at == 7:
-                    continue
+            for g in range(home + (at == 7), groups):
                 fr, fi = real[g], imag[g]
                 if g == home:
                     fr, fi = jnp.where(row > at, fr, 0.0), jnp.where(row > at, fi, 0.0)
                 for d, x, y in later:
                     panel[2 * d][g] = panel[2 * d][g] - (fr * x + fi * y)
                     panel[2 * d + 1][g] = panel[2 * d + 1][g] - (fi * x - fr * y)
-                if j < users - 1:
-                    a[g] = a[g] - (fr * pivot_row + fi * turned_row)
-                    if g < groups:
-                        ia[g] = ia[g] - (fr * turned_row - fi * pivot_row)
+                for x, ix, pivot_row, turned_row in pivots:
+                    x[g] = x[g] - (fr * pivot_row + fi * turned_row)
+                    ix[g] = ix[g] - (fr * turned_row - fi * pivot_row)
     upper = []
     for g in range(groups):
         diagonal = 2 * (row + 8 * g)
-        keep = (spot >= diagonal) & (spot != diagonal + 1)
+        keep = (lanes % width >= diagonal) & (lanes % width != diagonal + 1)
         upper.append(jnp.where(keep, a[g] * (by_row[g] * constellation_norm), 0.0))
-    return upper, [x * by_lane for x in a[groups:]]
+    return upper, [x * scale for x, scale in zip(q, by_row)]
 
 
 def kernel(
@@ -139,23 +129,35 @@
     )
     for copy in small:
         copy.start()
-    half, quarter, width, depth = users // 2, users // 4, 2 * users, 2 * (users + symbols)
+    half, quarter, width = users // 2, users // 4, 2 * users
+    tail = share * half + quarter
+    compact = 2 * symbols <= users
+    at, edge8 = iota((half, LANES), 1), iota((quarter, LANES), 1) // users
+    even = iota((users, LANES), 1) % 2 == 0
     sends = []
 
-    def fold(number, k, product):
-        slot = number % raw.shape[0]
-        raw[slot] = jnp.where(iota((depth, LANES), 1) < width, product[:depth], product[depth:])
-        on_even = raw[slot, pl.ds(0, depth // 2, stride=2), :]
-        on_odd = raw[slot, pl.ds(1, depth // 2, stride=2), :]
-        even = iota((depth // 2, LANES), 1) % 2 == 0
-        whole = pair_swap(on_odd) + jnp.where(even, on_even, -on_even)
-        part[k, :half] = whole[:half]
-        part[k, half : half + quarter] = jnp.where(
-            iota((quarter, LANES), 1) % width >= users,
-            whole[half + quarter : users],
-            pltpu.roll(whole[half : half + quarter], LANES - users, 1),
+    def fold(number, k, products):
+        lower = []
+        for s, product in enumerate(products):
+            slot = (number * share + s) % raw.shape[0]
+            raw[slot, :, : width + 2 * symbols] = product
+            on_even = raw[slot, pl.ds(0, users, stride=2), :]
+            on_odd = raw[slot, pl.ds(1, users, stride=2), :]
+            whole = pair_swap(on_odd) + jnp.where(even, on_even, -on_even)
+            lower.append(whole[half:])
+            upper = whole[:half]
+            if compact:
+                upper = jnp.where(at < 3 * users, upper, pltpu.roll(whole[half:], users, 1))
+            part[k, s * half : (s + 1) * half] = upper
+        part[k, share * half : tail] = jnp.where(
+            edge8 == 0, pltpu.roll(lower[1][:quarter], 3 * users, 1),
+            jnp.where(
+                edge8 == 1, lower[0][quarter:],
+                jnp.where(edge8 == 2, pltpu.roll(lower[0][:quarter], users, 1), pltpu.roll(lower[1][quarter:], width, 1)),
+            ),
         )
-        part[k, half + quarter :] = whole[users:]
+        if not compact:
+            part[k, tail:] = jnp.where(at < width, pltpu.roll(lower[0], width, 1), lower[1])
         if k:
             if number == 0:
                 pl.semaphore_wait(barrier, clusters + bands - 2)
@@ -166,17 +168,25 @@
             copy.start()
             sends.append(copy)
 
-    waiting = None
-    for number, k in enumerate(order):
-        for copy in loads[k]:
-            copy.wait()
-        fixed = jnp.concatenate([held[k, s, :width] for s in range(share)], axis=0)
-        streamed = jnp.concatenate([held[k, s] for s in range(share)], axis=0)
-        product = lax.dot_general(streamed, fixed, NT, preferred_element_type=jnp.float32)
-        if waiting:
-            fold(*waiting)
-        waiting = (number, k, product)
-    fold(*waiting)
+    raw[...] = jnp.zeros_like(raw)
+    waiting = []
+    numbered = list(enumerate(order))
+    for lot in [numbered[:1]] + [numbered[i : i + 2] for i in range(1, clusters, 2)]:
+        fresh = []
+        for number, k in lot:
+            for copy in loads[k]:
+                copy.wait()
+        for number, k in lot:
+            products = []
+            for s in range(share):
+                both = held[k, s]
+                products.append(lax.dot_general(both[:width], both, NT, preferred_element_type=jnp.float32))
+            fresh.append((number, k, products))
+        for chunk in waiting:
+            fold(*chunk)
+        waiting = fresh
+    for chunk in waiting:
+        fold(*chunk)
 
     for copy in small:
         copy.wait()
@@ -210,27 +220,37 @@
         jnp.sum(jnp.where(iota((1, bands), 1) == band, noise_ref[s : s + 1, :], 0.0), axis=1, keepdims=True)
         for s in range(share)
     ]
-    row, lanes = iota((8, LANES), 0), iota((8, LANES), 1)
+    row, lanes, extra = iota((8, LANES), 0), iota((8, LANES), 1), 2 * mine_t
     noise = jnp.where(lanes >= width, noises[1], noises[0])
     for copy in sends:
         copy.wait_recv()
     total = part[0]
     for k in range(1, clusters):
         total = total + came[k]
-    corner = total[half : half + quarter]
+    tile, ups = total[share * half : tail], [total[s * half : (s + 1) * half] for s in range(share)]
     inside = iota((quarter, LANES), 1) % width >= users
-    lower = [jnp.where(inside, x, 0.0) for x in (pltpu.roll(corner, users, 1), corner)]
-    mats = jnp.concatenate([total[:half]] + lower + [total[half + quarter :]], axis=0)
-    lines = [mats[8 * g : 8 * g + 8] for g in range((users + symbols) // 8)]
+    above = jnp.where(at < width, ups[0], pltpu.roll(ups[1], width, 1))
+    below = [jnp.where(inside, x, 0.0) for x in (pltpu.roll(tile, 3 * users, 1), tile)]
+    seen = [jnp.where(at < width, pltpu.roll(ups[0], width, 1), ups[1])]
+    if compact:
+        seen.append(jnp.where(at < width, pltpu.roll(ups[0], users, 1), pltpu.roll(ups[1], 3 * users, 1)))
+    else:
+        seen.append(total[tail:])
+    seen = [jnp.where(at % width < 2 * symbols, x, 0.0) for x in seen]
+    lines = [above[:8], above[8:]] + below
     for g in range(users // 8):
         lines[g] = jnp.where(lanes % width == 2 * (row + 8 * g), lines[g] + noise, lines[g])
-    upper, rotated = eliminate(lines, users)
-    upper, rotated = jnp.concatenate(upper, axis=0), jnp.concatenate(rotated, axis=0)
-    corner = jnp.where(inside, upper[half + quarter :], pltpu.roll(upper[half : half + quarter], LANES - users, 1))
+    upper, rotated = eliminate(lines, [x[8 * i : 8 * i + 8] for x in seen for i in range(half // 8)], users)
+    corner = jnp.where(inside, upper[3], pltpu.roll(upper[2], 3 * users, 1))
     for b in range(bands):
-        packed[b, :half] = upper[:half]
+        z = jnp.zeros_like(corner)
+        for g in range(users // 8):
+            shift = extra * (g - b) % LANES
+            z = jnp.where(lanes % width // extra == g, pltpu.roll(rotated[g], shift, 1) if shift else rotated[g], z)
+        packed[b, :8] = upper[0]
+        packed[b, 8:half] = upper[1]
         packed[b, half : half + quarter] = corner
-        packed[b, half + quarter :] = rotated[mine_t * b : mine_t * (b + 1)]
+        packed[b, half + quarter :] = z
     near = []
     inner = jnp.minimum(band, bands - 1 - band)
     outward = jnp.where(2 * band < bands - 1, 1, -1)
@@ -247,8 +267,9 @@
         copy.start()
         usends.append(copy)
 
-    r, c = iota((width, LANES), 0), iota((width, LANES), 1)
-    minus = jnp.where(c % width // 2 == r % users, -1.0, 0.0).astype(jnp.bfloat16)
+    r, c = iota((4 * rows, LANES), 0), iota((4 * rows, LANES), 1)
+    is_off = (r // rows) % 2
+    chosen = jnp.where(c % extra == 2 * (r % mine_t) + is_off, (2 * is_off - 1).astype(jnp.float32), 0.0).astype(jnp.bfloat16)
     sr, sc = iota((width, LANES), 0), iota((width, LANES), 1)
     suffix = [
         jnp.where((sr // users + 2 * h == sc // users) & (sr % users >= sc % users), 1.0 / users, 0.0).astype(jnp.bfloat16)
@@ -266,8 +287,6 @@
         straight = [(top, corner, pltpu.roll(corner, users, 1))]
         straight.append((pltpu.roll(top, width, 1), pltpu.roll(corner, width, 1), pltpu.roll(corner, 3 * users, 1)))
         z = box[b, half + quarter :]
-        low = pltpu.roll(z, width, 1)
-        low = low - low.astype(jnp.bfloat16).astype(jnp.float32)
         side, edge = iota(top.shape, 1) // width, iota(corner.shape, 1) // users
         for s in range(share):
             weights = []
@@ -278,17 +297,14 @@
                     jnp.where(edge == 2 * e + 1, third, 0.0),
                     jnp.where(edge == 2 * e + 1, fourth, 0.0),
                 ]
-            high, rest_of = split(jnp.concatenate(weights, axis=0))
-            zl = iota(z.shape, 1)
-            both = jnp.where(zl // width == s, z, low)
-            both = jnp.concatenate(
-                [jnp.concatenate([jnp.where(zl % 2 == o, both, 0.0)] * pieces, axis=0) for o in range(2)] * 2, axis=0
-            ).astype(jnp.bfloat16)
-            p = points[b, s]
-            rest = lax.dot_general(
-                jnp.concatenate([p, both], axis=1), jnp.concatenate([high, minus], axis=1), NT,
-                preferred_element_type=jnp.float32,
-            ) + lax.dot_general(p, rest_of, NT, preferred_element_type=jnp.float32)
+            own = [jnp.where(lanes // extra == width * s // extra + g, z, 0.0) for g in range(users // 8)]
+            high, low = split(
+                jnp.concatenate([jnp.concatenate(weights, axis=0), jnp.concatenate(own + own, axis=0)], axis=1)
+            )
+            p = jnp.concatenate([points[b, s], chosen], axis=1)
+            rest = lax.dot_general(p, high, NT, preferred_element_type=jnp.float32) + lax.dot_general(
+                p, low, NT, preferred_element_type=jnp.float32
+            )
             result = None
             for h in range(2):
                 on, off = rest[2 * h * rows : (2 * h + 1) * rows], rest[(2 * h + 1) * rows : (2 * h + 2) * rows]
@@ -307,9 +323,9 @@
     users, symbols = double_users // 2, observed_samples.shape[2] // 2
     share, mine_t = tones // clusters, symbols // bands
     pieces = retained_branches.shape[-1] // LANES
-    assert share == 2 and 4 * users == LANES
+    assert share == 2 and 4 * users == LANES and 4 * mine_t <= users // 2
     dims = (clusters, bands, users, symbols, share, mine_t, pieces)
-    lines = 3 * users // 4
+    lines = share * users // 2 + users // 4 + (0 if 2 * symbols <= users else users // 2)
     f32, bf16 = jnp.float32, jnp.bfloat16
     vmem, dma = pltpu.VMEM, pltpu.SemaphoreType.DMA
     return pl.pallas_call(
@@ -326,12 +342,12 @@
             vmem(disturbance_variance.shape[::-1], f32),
             vmem(retained_branches.shape, jnp.int32),
             vmem((clusters, share, 2 * (users + symbols), antennas), bf16),
-            vmem((2, 2 * (users + symbols), LANES), f32),
-            vmem((clusters, lines + symbols, LANES), f32),
-            vmem((clusters, lines + symbols, LANES), f32),
+            vmem((4, 2 * users, LANES), f32),
+            vmem((clusters, lines, LANES), f32),
+            vmem((clusters, lines, LANES), f32),
             vmem((bands, share, 4 * pieces * mine_t, LANES), bf16),
-            vmem((bands, lines + mine_t, LANES), f32),
-            vmem((bands, lines + mine_t, LANES), f32),
+            vmem((bands, users, LANES), f32),
+            vmem((bands, users, LANES), f32),
             dma((2,)), dma((2, clusters)), dma((clusters,)), dma((clusters,)), dma((bands,)), dma((bands,)),
         ],
         compiler_params=pltpu.CompilerParams(collective_id=0, has_side_effects=True),

time: 17.1 us -> 16.3 us (0.953)
  Pallas kernels: 16.3 us -> 15.5 us
    pallas_call x1, Pallas kernels: 16.3 us -> 15.5 us  [local(): pl.pallas_call(functools.partial(kernel, dims), out_shape=pltpu.VMEM(reta...]
where the time goes in v5:
time: 16.3 us; the launch traced here: 16.1 us
  Pallas kernels  15.5 us (95%)
  local copies, waits for them, and re-layouts  0.66 us (4%)
    pallas_call x1, Pallas kernels, local(): pl.pallas_call(functools.partial(kernel, dims), out_shape=pltpu.VMEM(reta...  15.5 us
    unnamed x1, local copies, waits for them, and re-layouts  0.66 us

profile of v5, /device:TPU:0, one launch (start us, length us, event | category | flops | bytes accessed | tf_op | source)
XLA Modules:
  0.0 16.1 jit_solution(10108104030738129184)
XLA Ops:
  0.0 15.5 %detect.1 = f32[4,2,4,1024]{3,2,1,0:T(4,128)S(1)} custom-call(f32[2,4]{1,0:T(2,128)} %bitcast.1, bf16[1,16,64,1024]{3,2,1,0:T(8,128)(2,1)} %gains_ref.1, bf16[1,16,32,1024]{3,2,1,0:T(8,128)(2,1)} %samples_ref.1, s32[4,2,4,1024]{3,2,1,0:T(4,128)} %branches_any.1), custom_call_target="tpu_custom_call" | custom-call | tf_op jit(solution)/shard_map/detect/pallas_call | solution.py:331
  15.5 0.7 %copy.6 = f32[4,2,4,1024]{3,2,1,0:T(4,128)} copy(f32[4,2,4,1024]{3,2,1,0:T(4,128)S(1)} %detect.1) | data formatting | bytes 262144

commit v6 on v5

--- a/solution.py
+++ b/solution.py
@@ -101,6 +101,7 @@
     for k in range(1, bands):
         pl.semaphore_signal(barrier, inc=1, device_id={"par": lax.rem(band + k, bands)}, device_id_type=MESH)
 
+    far, mid = clusters // 2, clusters // 4
     order = list(range(clusters - 1, -1, -1))
     peers = {}
     for k in order:
@@ -287,6 +288,7 @@
         straight = [(top, corner, pltpu.roll(corner, users, 1))]
         straight.append((pltpu.roll(top, width, 1), pltpu.roll(corner, width, 1), pltpu.roll(corner, 3 * users, 1)))
         z = box[b, half + quarter :]
+        rests = []
         side, edge = iota(top.shape, 1) // width, iota(corner.shape, 1) // users
         for s in range(share):
             weights = []
@@ -305,6 +307,8 @@
             rest = lax.dot_general(p, high, NT, preferred_element_type=jnp.float32) + lax.dot_general(
                 p, low, NT, preferred_element_type=jnp.float32
             )
+            rests.append(rest)
+        for s, rest in enumerate(rests):
             result = None
             for h in range(2):
                 on, off = rest[2 * h * rows : (2 * h + 1) * rows], rest[(2 * h + 1) * rows : (2 * h + 2) * rows]

time: 16.3 us -> 16.1 us (0.988)
  Pallas kernels: 15.5 us -> 15.2 us
    pallas_call x1, Pallas kernels: 15.5 us -> 15.2 us  [local(): pl.pallas_call(functools.partial(kernel, dims), out_shape=pltpu.VMEM(reta...]
where the time goes in v6:
time: 16.1 us; the launch traced here: 15.9 us
  Pallas kernels  15.2 us (94%)
  local copies, waits for them, and re-layouts  0.66 us (4%)
    pallas_call x1, Pallas kernels, local(): pl.pallas_call(functools.partial(kernel, dims), out_shape=pltpu.VMEM(reta...  15.2 us
    unnamed x1, local copies, waits for them, and re-layouts  0.66 us

profile of v6, /device:TPU:0, one launch (start us, length us, event | category | flops | bytes accessed | tf_op | source)
XLA Modules:
  0.0 15.9 jit_solution(15762959167783550537)
XLA Ops:
  0.0 15.2 %detect.1 = f32[4,2,4,1024]{3,2,1,0:T(4,128)S(1)} custom-call(f32[2,4]{1,0:T(2,128)} %bitcast.1, bf16[1,16,64,1024]{3,2,1,0:T(8,128)(2,1)} %gains_ref.1, bf16[1,16,32,1024]{3,2,1,0:T(8,128)(2,1)} %samples_ref.1, s32[4,2,4,1024]{3,2,1,0:T(4,128)} %branches_any.1), custom_call_target="tpu_custom_call" | custom-call | tf_op jit(solution)/shard_map/detect/pallas_call | solution.py:335
  15.3 0.7 %copy.6 = f32[4,2,4,1024]{3,2,1,0:T(4,128)} copy(f32[4,2,4,1024]{3,2,1,0:T(4,128)S(1)} %detect.1) | data formatting | bytes 262144

commit v7 on v6

--- a/solution.py
+++ b/solution.py
@@ -115,10 +115,10 @@
         tones = pl.ds(peers[k] * share, share)
         loads[k] = (
             pltpu.make_async_copy(
-                gains_ref.at[0, tones], held.at[k, :, pl.ds(0, 2 * users)], load_sem.at[0, k]
+                gains_ref.at[0, tones], held.at[k, :, pl.ds(0, 2 * users)], load_sem.at[k]
             ),
             pltpu.make_async_copy(
-                samples_ref.at[0, tones], held.at[k, :, pl.ds(2 * users, 2 * symbols)], load_sem.at[1, k]
+                samples_ref.at[0, tones], held.at[k, :, pl.ds(2 * users, 2 * symbols)], load_sem.at[k]
             ),
         )
         for copy in loads[k]:
@@ -135,7 +135,7 @@
     compact = 2 * symbols <= users
     at, edge8 = iota((half, LANES), 1), iota((quarter, LANES), 1) // users
     even = iota((users, LANES), 1) % 2 == 0
-    sends = []
+    sends, ready = [], []
 
     def fold(number, k, products):
         lower = []
@@ -146,9 +146,13 @@
             on_odd = raw[slot, pl.ds(1, users, stride=2), :]
             whole = pair_swap(on_odd) + jnp.where(even, on_even, -on_even)
             lower.append(whole[half:])
-            upper = whole[:half]
-            if compact:
-                upper = jnp.where(at < 3 * users, upper, pltpu.roll(whole[half:], users, 1))
+            upper, bottom = whole[:half], whole[half:]
+            if s:
+                upper = pltpu.roll(upper, width, 1)
+                if compact:
+                    upper = jnp.where((at >= users) & (at < width), pltpu.roll(bottom, 3 * users, 1), upper)
+            elif compact:
+                upper = jnp.where(at < 3 * users, upper, pltpu.roll(bottom, users, 1))
             part[k, s * half : (s + 1) * half] = upper
         part[k, share * half : tail] = jnp.where(
             edge8 == 0, pltpu.roll(lower[1][:quarter], 3 * users, 1),
@@ -160,14 +164,21 @@
         if not compact:
             part[k, tail:] = jnp.where(at < width, pltpu.roll(lower[0], width, 1), lower[1])
         if k:
-            if number == 0:
+            ready.append(
+                pltpu.make_async_remote_copy(
+                    src_ref=part.at[k], dst_ref=came.at[k], send_sem=send_sem.at[0], recv_sem=recv_sem.at[0],
+                    device_id={"chain": peers[k]}, device_id_type=MESH,
+                )
+            )
+
+    def post(last):
+        if ready and (sends or last >= 0):
+            if not sends:
                 pl.semaphore_wait(barrier, clusters + bands - 2)
-            copy = pltpu.make_async_remote_copy(
-                src_ref=part.at[k], dst_ref=came.at[k], send_sem=send_sem.at[k], recv_sem=recv_sem.at[k],
-                device_id={"chain": peers[k]}, device_id_type=MESH,
-            )
-            copy.start()
-            sends.append(copy)
+            for copy in ready:
+                copy.start()
+            sends.extend(ready)
+            ready.clear()
 
     raw[...] = jnp.zeros_like(raw)
     waiting = []
@@ -175,8 +186,7 @@
     for lot in [numbered[:1]] + [numbered[i : i + 2] for i in range(1, clusters, 2)]:
         fresh = []
         for number, k in lot:
-            for copy in loads[k]:
-                copy.wait()
+            pltpu.make_async_copy(held.at[k], held.at[k], load_sem.at[k]).wait()
         for number, k in lot:
             products = []
             for s in range(share):
@@ -185,9 +195,11 @@
             fresh.append((number, k, products))
         for chunk in waiting:
             fold(*chunk)
+        post(lot[0][0] - 1)
         waiting = fresh
     for chunk in waiting:
         fold(*chunk)
+    post(clusters)
 
     for copy in small:
         copy.wait()
@@ -223,20 +235,19 @@
     ]
     row, lanes, extra = iota((8, LANES), 0), iota((8, LANES), 1), 2 * mine_t
     noise = jnp.where(lanes >= width, noises[1], noises[0])
-    for copy in sends:
-        copy.wait_recv()
+    every = pltpu.make_async_remote_copy(
+        src_ref=part.at[pl.ds(1, clusters - 1)], dst_ref=came.at[pl.ds(1, clusters - 1)], send_sem=send_sem.at[0],
+        recv_sem=recv_sem.at[0], device_id={"chain": peers[1]}, device_id_type=MESH,
+    )
+    every.wait_recv()
     total = part[0]
     for k in range(1, clusters):
         total = total + came[k]
     tile, ups = total[share * half : tail], [total[s * half : (s + 1) * half] for s in range(share)]
     inside = iota((quarter, LANES), 1) % width >= users
-    above = jnp.where(at < width, ups[0], pltpu.roll(ups[1], width, 1))
+    above, heard = jnp.where(at < width, ups[0], ups[1]), jnp.where(at < width, ups[1], ups[0])
     below = [jnp.where(inside, x, 0.0) for x in (pltpu.roll(tile, 3 * users, 1), tile)]
-    seen = [jnp.where(at < width, pltpu.roll(ups[0], width, 1), ups[1])]
-    if compact:
-        seen.append(jnp.where(at < width, pltpu.roll(ups[0], users, 1), pltpu.roll(ups[1], 3 * users, 1)))
-    else:
-        seen.append(total[tail:])
+    seen = [pltpu.roll(heard, width, 1), pltpu.roll(heard, users, 1) if compact else total[tail:]]
     seen = [jnp.where(at % width < 2 * symbols, x, 0.0) for x in seen]
     lines = [above[:8], above[8:]] + below
     for g in range(users // 8):
@@ -246,8 +257,9 @@
     for b in range(bands):
         z = jnp.zeros_like(corner)
         for g in range(users // 8):
-            shift = extra * (g - b) % LANES
-            z = jnp.where(lanes % width // extra == g, pltpu.roll(rotated[g], shift, 1) if shift else rotated[g], z)
+            slot = (b + g + 1 - users // 8) % (width // extra)
+            shift = extra * (slot - b) % LANES
+            z = jnp.where(lanes % width // extra == slot, pltpu.roll(rotated[g], shift, 1) if shift else rotated[g], z)
         packed[b, :8] = upper[0]
         packed[b, 8:half] = upper[1]
         packed[b, half : half + quarter] = corner
@@ -262,7 +274,7 @@
     for i in range(bands - 1, 0, -1):
         peer = near[i - 1]
         copy = pltpu.make_async_remote_copy(
-            src_ref=packed.at[peer], dst_ref=taken.at[band], send_sem=usend_sem.at[i], recv_sem=urecv_sem.at[band],
+            src_ref=packed.at[peer], dst_ref=taken.at[band], send_sem=usend_sem.at[0], recv_sem=urecv_sem.at[band],
             device_id={"par": peer}, device_id_type=MESH,
         )
         copy.start()
@@ -271,6 +283,7 @@
     r, c = iota((4 * rows, LANES), 0), iota((4 * rows, LANES), 1)
     is_off = (r // rows) % 2
     chosen = jnp.where(c % extra == 2 * (r % mine_t) + is_off, (2 * is_off - 1).astype(jnp.float32), 0.0).astype(jnp.bfloat16)
+    slots = [lax.rem(band + g + 1 + (width // extra) - users // 8, width // extra) for g in range(users // 8)]
     sr, sc = iota((width, LANES), 0), iota((width, LANES), 1)
     suffix = [
         jnp.where((sr // users + 2 * h == sc // users) & (sr % users >= sc % users), 1.0 / users, 0.0).astype(jnp.bfloat16)
@@ -280,7 +293,7 @@
         b = band if i == 0 else near[i - 1]
         if i:
             pltpu.make_async_remote_copy(
-                src_ref=packed.at[b], dst_ref=taken.at[b], send_sem=usend_sem.at[i], recv_sem=urecv_sem.at[b],
+                src_ref=packed.at[b], dst_ref=taken.at[b], send_sem=usend_sem.at[0], recv_sem=urecv_sem.at[b],
                 device_id={"par": b}, device_id_type=MESH,
             ).wait_recv()
         box = taken if i else packed
@@ -299,7 +312,9 @@
                     jnp.where(edge == 2 * e + 1, third, 0.0),
                     jnp.where(edge == 2 * e + 1, fourth, 0.0),
                 ]
-            own = [jnp.where(lanes // extra == width * s // extra + g, z, 0.0) for g in range(users // 8)]
+            own = [
+                jnp.where(lanes // extra == width * s // extra + slots[g], z, 0.0) for g in range(users // 8)
+            ]
             high, low = split(
                 jnp.concatenate([jnp.concatenate(weights, axis=0), jnp.concatenate(own + own, axis=0)], axis=1)
             )
@@ -317,8 +332,11 @@
                     result = step if result is None else result + step
             for r in range(pieces):
                 out_ref[b, s, :, LANES * r : LANES * (r + 1)] = result[mine_t * r : mine_t * (r + 1)]
-    for copy in sends + usends:
-        copy.wait_send()
+    every.wait_send()
+    pltpu.make_async_remote_copy(
+        src_ref=packed.at[pl.ds(1, bands - 1)], dst_ref=taken.at[pl.ds(1, bands - 1)], send_sem=usend_sem.at[0],
+        recv_sem=urecv_sem.at[0], device_id={"par": near[0]}, device_id_type=MESH,
+    ).wait_send()
 
 
 def local(propagation_gains, observed_samples, disturbance_variance, retained_branches):
@@ -352,7 +370,7 @@
             vmem((bands, share, 4 * pieces * mine_t, LANES), bf16),
             vmem((bands, users, LANES), f32),
             vmem((bands, users, LANES), f32),
-            dma((2,)), dma((2, clusters)), dma((clusters,)), dma((clusters,)), dma((bands,)), dma((bands,)),
+            dma((2,)), dma((clusters,)), dma((1,)), dma((1,)), dma((1,)), dma((bands,)),
         ],
         compiler_params=pltpu.CompilerParams(collective_id=0, has_side_effects=True),
         name="detect",

time: 16.1 us -> 15.6 us (0.969)
  Pallas kernels: 15.2 us -> 14.8 us
    pallas_call x1, Pallas kernels: 15.2 us -> 14.8 us  [local(): pl.pallas_call(functools.partial(kernel, dims), out_shape=pltpu.VMEM(reta...]
where the time goes in v7:
time: 15.6 us; the launch traced here: 15.5 us
  Pallas kernels  14.8 us (95%)
  local copies, waits for them, and re-layouts  0.66 us (4%)
    pallas_call x1, Pallas kernels, local(): pl.pallas_call(functools.partial(kernel, dims), out_shape=pltpu.VMEM(reta...  14.8 us
    unnamed x1, local copies, waits for them, and re-layouts  0.66 us

profile of v7, /device:TPU:0, one launch (start us, length us, event | category | flops | bytes accessed | tf_op | source)
XLA Modules:
  0.0 15.5 jit_solution(243117126618741588)
XLA Ops:
  0.0 14.8 %detect.1 = f32[4,2,4,1024]{3,2,1,0:T(4,128)S(1)} custom-call(f32[2,4]{1,0:T(2,128)} %bitcast.1, bf16[1,16,64,1024]{3,2,1,0:T(8,128)(2,1)} %gains_ref.1, bf16[1,16,32,1024]{3,2,1,0:T(8,128)(2,1)} %samples_ref.1, s32[4,2,4,1024]{3,2,1,0:T(4,128)} %branches_any.1), custom_call_target="tpu_custom_call" | custom-call | tf_op jit(solution)/shard_map/detect/pallas_call | solution.py:353
  14.8 0.7 %copy.6 = f32[4,2,4,1024]{3,2,1,0:T(4,128)} copy(f32[4,2,4,1024]{3,2,1,0:T(4,128)S(1)} %detect.1) | data formatting | bytes 262144

commit v8 on v7

--- a/solution.py
+++ b/solution.py
@@ -17,8 +17,7 @@
 
 
 def panels(users):
-    wide = users // 2
-    return [(j, 4) for j in range(0, wide, 4)] + [(j, 8) for j in range(wide, users, 8)]
+    return [(0, 4), (4, 4)] + [(j, 8) for j in range(8, users, 8)]
 
 
 def split(x):
@@ -95,12 +94,6 @@
     clusters, bands, users, symbols, share, mine_t, pieces = dims
     me, band = lax.axis_index("chain"), lax.axis_index("par")
 
-    barrier = pltpu.get_barrier_semaphore()
-    for k in range(1, clusters):
-        pl.semaphore_signal(barrier, inc=1, device_id={"chain": lax.rem(me + k, clusters)}, device_id_type=MESH)
-    for k in range(1, bands):
-        pl.semaphore_signal(barrier, inc=1, device_id={"par": lax.rem(band + k, bands)}, device_id_type=MESH)
-
     far, mid = clusters // 2, clusters // 4
     order = list(range(clusters - 1, -1, -1))
     peers = {}
@@ -110,19 +103,20 @@
             digit = lax.rem(me // bit, 2)
             peers[k] = peers[k] + bit * (1 - digit if (k // bit) % 2 else digit)
             bit *= 2
-    loads = {}
-    for k in order:
+    def load(k):
         tones = pl.ds(peers[k] * share, share)
-        loads[k] = (
-            pltpu.make_async_copy(
-                gains_ref.at[0, tones], held.at[k, :, pl.ds(0, 2 * users)], load_sem.at[k]
-            ),
-            pltpu.make_async_copy(
-                samples_ref.at[0, tones], held.at[k, :, pl.ds(2 * users, 2 * symbols)], load_sem.at[k]
-            ),
-        )
-        for copy in loads[k]:
-            copy.start()
+        pltpu.make_async_copy(gains_ref.at[0, tones], held.at[k, :, pl.ds(0, 2 * users)], load_sem.at[k]).start()
+        pltpu.make_async_copy(
+            samples_ref.at[0, tones], held.at[k, :, pl.ds(2 * users, 2 * symbols)], load_sem.at[k]
+        ).start()
+
+    for k in order[:clusters]:
+        load(k)
+    barrier = pltpu.get_barrier_semaphore()
+    for k in range(1, clusters):
+        pl.semaphore_signal(barrier, inc=1, device_id={"chain": lax.rem(me + k, clusters)}, device_id_type=MESH)
+    for k in range(1, bands):
+        pl.semaphore_signal(barrier, inc=1, device_id={"par": lax.rem(band + k, bands)}, device_id_type=MESH)
 
     small = (
         pltpu.make_async_copy(noise_any, noise_ref, small_sem.at[0]),

time: 15.6 us -> 15.5 us (level)
    pallas_call x1, Pallas kernels: 14.8 us -> 14.7 us  [local(): pl.pallas_call(functools.partial(kernel, dims), out_shape=pltpu.VMEM(reta...]
where the time goes in v8:
time: 15.5 us; the launch traced here: 15.3 us
  Pallas kernels  14.7 us (95%)
  local copies, waits for them, and re-layouts  0.66 us (4%)
    pallas_call x1, Pallas kernels, local(): pl.pallas_call(functools.partial(kernel, dims), out_shape=pltpu.VMEM(reta...  14.7 us
    unnamed x1, local copies, waits for them, and re-layouts  0.66 us

profile of v8, /device:TPU:0, one launch (start us, length us, event | category | flops | bytes accessed | tf_op | source)
XLA Modules:
  0.0 15.3 jit_solution(12375238409056048729)
XLA Ops:
  0.0 14.7 %detect.1 = f32[4,2,4,1024]{3,2,1,0:T(4,128)S(1)} custom-call(f32[2,4]{1,0:T(2,128)} %bitcast.1, bf16[1,16,64,1024]{3,2,1,0:T(8,128)(2,1)} %gains_ref.1, bf16[1,16,32,1024]{3,2,1,0:T(8,128)(2,1)} %samples_ref.1, s32[4,2,4,1024]{3,2,1,0:T(4,128)} %branches_any.1), custom_call_target="tpu_custom_call" | custom-call | tf_op jit(solution)/shard_map/detect/pallas_call | solution.py:347
  14.7 0.7 %copy.6 = f32[4,2,4,1024]{3,2,1,0:T(4,128)} copy(f32[4,2,4,1024]{3,2,1,0:T(4,128)S(1)} %detect.1) | data formatting | bytes 262144

commit v9 on v8

--- a/solution.py
+++ b/solution.py
@@ -89,7 +89,7 @@
 def kernel(
     dims, noise_any, gains_ref, samples_ref, branches_any, out_ref,
     noise_ref, branches_ref, held, raw, part, came, points, packed, taken,
-    small_sem, load_sem, send_sem, recv_sem, usend_sem, urecv_sem,
+    small_sem, load_sem, send_sem, recv_sem, urecv_sem,
 ):
     clusters, bands, users, symbols, share, mine_t, pieces = dims
     me, band = lax.axis_index("chain"), lax.axis_index("par")
@@ -105,9 +105,9 @@
             bit *= 2
     def load(k):
         tones = pl.ds(peers[k] * share, share)
-        pltpu.make_async_copy(gains_ref.at[0, tones], held.at[k, :, pl.ds(0, 2 * users)], load_sem.at[k]).start()
+        pltpu.make_async_copy(gains_ref.at[0, tones], held.at[k, :, pl.ds(0, 2 * users)], load_sem.at[(k + 1) // 2]).start()
         pltpu.make_async_copy(
-            samples_ref.at[0, tones], held.at[k, :, pl.ds(2 * users, 2 * symbols)], load_sem.at[k]
+            samples_ref.at[0, tones], held.at[k, :, pl.ds(2 * users, 2 * symbols)], load_sem.at[(k + 1) // 2]
         ).start()
 
     for k in order[:clusters]:
@@ -179,8 +179,8 @@
     numbered = list(enumerate(order))
     for lot in [numbered[:1]] + [numbered[i : i + 2] for i in range(1, clusters, 2)]:
         fresh = []
-        for number, k in lot:
-            pltpu.make_async_copy(held.at[k], held.at[k], load_sem.at[k]).wait()
+        landed = held.at[pl.ds(lot[-1][1], len(lot))]
+        pltpu.make_async_copy(landed, landed, load_sem.at[(lot[0][1] + 1) // 2]).wait()
         for number, k in lot:
             products = []
             for s in range(share):
@@ -268,7 +268,7 @@
     for i in range(bands - 1, 0, -1):
         peer = near[i - 1]
         copy = pltpu.make_async_remote_copy(
-            src_ref=packed.at[peer], dst_ref=taken.at[band], send_sem=usend_sem.at[0], recv_sem=urecv_sem.at[band],
+            src_ref=packed.at[peer], dst_ref=taken.at[band], send_sem=load_sem.at[0], recv_sem=urecv_sem.at[band],
             device_id={"par": peer}, device_id_type=MESH,
         )
         copy.start()
@@ -287,7 +287,7 @@
         b = band if i == 0 else near[i - 1]
         if i:
             pltpu.make_async_remote_copy(
-                src_ref=packed.at[b], dst_ref=taken.at[b], send_sem=usend_sem.at[0], recv_sem=urecv_sem.at[b],
+                src_ref=packed.at[b], dst_ref=taken.at[b], send_sem=load_sem.at[0], recv_sem=urecv_sem.at[b],
                 device_id={"par": b}, device_id_type=MESH,
             ).wait_recv()
         box = taken if i else packed
@@ -328,7 +328,7 @@
                 out_ref[b, s, :, LANES * r : LANES * (r + 1)] = result[mine_t * r : mine_t * (r + 1)]
     every.wait_send()
     pltpu.make_async_remote_copy(
-        src_ref=packed.at[pl.ds(1, bands - 1)], dst_ref=taken.at[pl.ds(1, bands - 1)], send_sem=usend_sem.at[0],
+        src_ref=packed.at[pl.ds(1, bands - 1)], dst_ref=taken.at[pl.ds(1, bands - 1)], send_sem=load_sem.at[0],
         recv_sem=urecv_sem.at[0], device_id={"par": near[0]}, device_id_type=MESH,
     ).wait_send()
 
@@ -364,7 +364,7 @@
             vmem((bands, share, 4 * pieces * mine_t, LANES), bf16),
             vmem((bands, users, LANES), f32),
             vmem((bands, users, LANES), f32),
-            dma((2,)), dma((clusters,)), dma((1,)), dma((1,)), dma((1,)), dma((bands,)),
+            dma((2,)), dma((clusters // 2 + 1,)), dma((1,)), dma((1,)), dma((bands,)),
         ],
         compiler_params=pltpu.CompilerParams(collective_id=0, has_side_effects=True),
         name="detect",

time: 15.5 us -> 15.4 us (level)
  no operation moved by 1% of the time
where the time goes in v9:
time: 15.4 us; the launch traced here: 15.3 us
  Pallas kernels  14.6 us (95%)
  local copies, waits for them, and re-layouts  0.66 us (4%)
    pallas_call x1, Pallas kernels, local(): pl.pallas_call(functools.partial(kernel, dims), out_shape=pltpu.VMEM(reta...  14.6 us
    unnamed x1, local copies, waits for them, and re-layouts  0.66 us

profile of v9, /device:TPU:0, one launch (start us, length us, event | category | flops | bytes accessed | tf_op | source)
XLA Modules:
  0.0 15.3 jit_solution(2183984222426120151)
XLA Ops:
  0.0 14.6 %detect.1 = f32[4,2,4,1024]{3,2,1,0:T(4,128)S(1)} custom-call(f32[2,4]{1,0:T(2,128)} %bitcast.1, bf16[1,16,64,1024]{3,2,1,0:T(8,128)(2,1)} %gains_ref.1, bf16[1,16,32,1024]{3,2,1,0:T(8,128)(2,1)} %samples_ref.1, s32[4,2,4,1024]{3,2,1,0:T(4,128)} %branches_any.1), custom_call_target="tpu_custom_call" | custom-call | tf_op jit(solution)/shard_map/detect/pallas_call | solution.py:347
  14.6 0.7 %copy.6 = f32[4,2,4,1024]{3,2,1,0:T(4,128)} copy(f32[4,2,4,1024]{3,2,1,0:T(4,128)S(1)} %detect.1) | data formatting | bytes 262144
